TPU v7x, 32 devices: a whole 2x2x4 slice. The times are simulated.
32 devices in a mesh: data: 8 (over z, y), model: 4 (over x, core).
Axes of the slice: x: 2, y: 2, z: 4, core: 2. Of those that a mesh axis runs over, the one named last changes fastest.
Arguments:
- tokens: bfloat16 [12288, 2048], P('data')
- w_query: bfloat16 [2048, 2048], P('data', 'model')
- w_kv: bfloat16 [2048, 512], P('data')
- w_out: bfloat16 [2048, 2048], P('model', 'data')
- ln_gain: float32 [2048], replicated
- positions: int32 [128], replicated
- grad_out: bfloat16 [12288, 2048], P('data')
Outputs:
- output 1: bfloat16 [12288, 2048], P('data')
- output 2: bfloat16 [12288, 2048], P('data')
- output 3: bfloat16 [2048, 2048], P('data', 'model')
- output 4: bfloat16 [2048, 512], P('data')
- output 5: bfloat16 [2048, 2048], P('model', 'data')
All inputs are finite; a program needn't handle non-finite values.
Results may differ from a plain program's by a relative error of at most 0.0139353.
Values are sent between devices in bfloat16 or wider.
A program may use at most 1 GiB of HBM per device.

v0:
```python
import jax
import jax.numpy as jnp
from jax import lax
from jax.sharding import PartitionSpec as P

NORM_EPS = 1e-6


def norm_rows(tok_rows):
    rows_f = tok_rows.astype(jnp.float32)
    centred = rows_f - jnp.mean(rows_f, axis=-1, keepdims=True)
    inv_std = lax.rsqrt(jnp.mean(centred * centred, axis=-1, keepdims=True) + NORM_EPS)
    return centred * inv_std, inv_std


def attend_fwd(queries, key_vals, visible):
    head_dim = queries.shape[-1]
    scores = jnp.einsum("bqhe,bke->bhqk", queries, key_vals[:, :, :head_dim], preferred_element_type=jnp.float32) * head_dim ** -0.5
    probs = jax.nn.softmax(jnp.where(visible, scores, -1e30), axis=-1)
    probs_b = probs.astype(jnp.bfloat16)
    mixed = jnp.einsum("bhqk,bke->bqhe", probs_b, key_vals[:, :, head_dim:], preferred_element_type=jnp.float32).astype(jnp.bfloat16)
    return mixed, probs, probs_b


def attend_bwd(queries, key_vals, probs, probs_b, grad_mixed):
    head_dim = queries.shape[-1]
    keys_b = key_vals[:, :, :head_dim]
    grad_probs = jnp.einsum("bqhe,bke->bhqk", grad_mixed, key_vals[:, :, head_dim:], preferred_element_type=jnp.float32)
    grad_vals = jnp.einsum("bhqk,bqhe->bke", probs_b, grad_mixed, preferred_element_type=jnp.float32)
    grad_scores = probs * (grad_probs - jnp.sum(probs * grad_probs, axis=-1, keepdims=True))
    grad_scores = (grad_scores * head_dim ** -0.5).astype(jnp.bfloat16)
    grad_query = jnp.einsum("bhqk,bke->bqhe", grad_scores, keys_b, preferred_element_type=jnp.float32).astype(jnp.bfloat16)
    grad_keys = jnp.einsum("bhqk,bqhe->bke", grad_scores, queries, preferred_element_type=jnp.float32)
    return grad_query, jnp.concatenate([grad_keys, grad_vals], axis=-1)


def solution(mesh):
    model_size = mesh.shape["model"]

    def device_step(tok_blk, q_weight_blk, kv_weight_blk, o_weight_blk, ln_gain, positions, grad_blk):
        tok_count = tok_blk.shape[0]
        seq_len = positions.shape[0]
        head_dim = kv_weight_blk.shape[1] // 2
        local_width = q_weight_blk.shape[1]
        seq_count = tok_count // seq_len
        part_rows = tok_count // model_size
        row_start = lax.axis_index("model") * part_rows
        visible = positions[None, :] <= positions[:, None]

        q_weight = lax.all_gather(q_weight_blk, "data", axis=0, tiled=True)
        kv_weight = lax.all_gather(kv_weight_blk, "data", axis=0, tiled=True)
        o_weight = lax.all_gather(o_weight_blk, "data", axis=1, tiled=True)

        normed, inv_std = norm_rows(tok_blk)
        hidden = (normed * ln_gain).astype(jnp.bfloat16)
        queries = jnp.dot(hidden, q_weight, preferred_element_type=jnp.float32).astype(jnp.bfloat16)
        queries = queries.reshape(seq_count, seq_len, local_width // head_dim, head_dim)
        hidden_part = lax.dynamic_slice_in_dim(hidden, row_start, part_rows, axis=0)
        kv_part = jnp.dot(hidden_part, kv_weight, preferred_element_type=jnp.float32).astype(jnp.bfloat16)
        key_vals = lax.all_gather(kv_part, "model", axis=0, tiled=True).reshape(seq_count, seq_len, 2 * head_dim)
        mixed, probs, probs_b = attend_fwd(queries, key_vals, visible)
        mixed = mixed.reshape(tok_count, local_width)
        attn_out = lax.psum(jnp.dot(mixed, o_weight, preferred_element_type=jnp.float32), "model").astype(jnp.bfloat16)

        grad_mixed = jnp.einsum("td,ed->te", grad_blk, o_weight, preferred_element_type=jnp.float32).astype(jnp.bfloat16)
        grad_o_part = jnp.einsum("te,td->ed", mixed, grad_blk, preferred_element_type=jnp.float32)
        grad_w_out = lax.psum_scatter(grad_o_part, "data", scatter_dimension=1, tiled=True).astype(jnp.bfloat16)
        grad_query, grad_kv = attend_bwd(queries, key_vals, probs, probs_b, grad_mixed.reshape(queries.shape))
        grad_query = grad_query.reshape(tok_count, local_width)
        grad_kv_part = lax.psum_scatter(grad_kv.reshape(tok_count, 2 * head_dim), "model", scatter_dimension=0, tiled=True).astype(jnp.bfloat16)
        grad_hidden = lax.psum_scatter(jnp.einsum("te,de->td", grad_query, q_weight, preferred_element_type=jnp.float32), "model", scatter_dimension=0, tiled=True)
        grad_hidden = grad_hidden + jnp.einsum("tc,dc->td", grad_kv_part, kv_weight, preferred_element_type=jnp.float32)
        grad_q_part = jnp.einsum("td,te->de", hidden, grad_query, preferred_element_type=jnp.float32)
        grad_w_query = lax.psum_scatter(grad_q_part, "data", scatter_dimension=0, tiled=True).astype(jnp.bfloat16)
        grad_kv_w = jnp.einsum("td,tc->dc", hidden_part, grad_kv_part, preferred_element_type=jnp.float32)
        grad_kv_w = lax.psum_scatter(grad_kv_w, "data", scatter_dimension=0, tiled=True)
        grad_w_kv = lax.psum(grad_kv_w, "model").astype(jnp.bfloat16)

        normed_part = lax.dynamic_slice_in_dim(normed, row_start, part_rows, axis=0)
        inv_std_part = lax.dynamic_slice_in_dim(inv_std, row_start, part_rows, axis=0)
        grad_normed = grad_hidden * ln_gain
        grad_tok_part = inv_std_part * (grad_normed - jnp.mean(grad_normed, axis=-1, keepdims=True) - normed_part * jnp.mean(grad_normed * normed_part, axis=-1, keepdims=True))
        grad_tokens = lax.all_gather(grad_tok_part.astype(jnp.bfloat16), "model", axis=0, tiled=True)
        return attn_out, grad_tokens, grad_w_query, grad_w_kv, grad_w_out

    return jax.shard_map(
        device_step,
        mesh=mesh,
        in_specs=(P("data", None), P("data", "model"), P("data", None), P("model", "data"), P(), P(), P("data", None)),
        out_specs=(P("data", None), P("data", None), P("data", "model"), P("data", None), P("model", "data")),
        check_vma=False,
    )
```

profile of v0, /device:TPU:0, one launch (start us, length us, event | category | flops | bytes accessed | tf_op | source)
XLA Modules:
  0.0 888.7 jit_solution(11530516046270885107)
XLA Ops:
  7.2 0.0 all-gather.6.cloned.1.call-start
  7.2 0.7 all-gather.6.cloned.1.call-update
  7.9 0.0 all-gather.12.cloned.1.call-start
  7.9 0.7 all-gather.12.cloned.1.call-update
  8.6 0.0 all-gather.10.cloned.1.call-start
  8.7 0.7 all-gather.10.cloned.1.call-update
  9.4 0.0 all-gather.8.cloned.1.call-start
  9.4 3.8 convert_reduce_fusion
  13.3 0.8 copy-done
  14.0 1.8 fusion.4
  15.8 7.3 fusion.2
  23.2 38.9 %all-gather.6.cloned.1.call-done = bf16[2048,512]{1,0:T(8,128)(2,1)} async-done(((bf16[256,512]{1,0:T(8,128)(2,1)}), bf16[2048,512]{1,0:T(8,128)(2,1)}) %all-gather.6.cloned.1.call-update) | async-done | bytes 2097168 | tf_op jit(solution)/shard_map/all_gather | solution.py:51
  62.1 3.8 fusion.21
  65.9 0.0 all-gather.8.cloned.1.call-update
  65.9 0.2 reduce-scatter.8.cloned.1.call-start
  66.2 0.1 broadcast_compare_fusion
  66.3 46.9 %all-gather.12.cloned.1.call-done = bf16[512,2048]{1,0:T(8,128)(2,1)} async-done(((bf16[512,256]{1,0:T(8,128)(2,1)}), bf16[512,2048]{1,0:T(8,128)(2,1)}) %all-gather.12.cloned.1.call-update) | async-done | bytes 2097168 | tf_op jit(solution)/shard_map/all_gather | solution.py:52
  113.1 6.9 convolution_convert_fusion
  120.0 0.4 reshape.72
  120.5 42.4 %all-gather.10.cloned.1.call-done = bf16[2048,512]{1,0:T(8,128)(2,1)} async-done(((bf16[256,512]{1,0:T(8,128)(2,1)}), bf16[2048,512]{1,0:T(8,128)(2,1)}) %all-gather.10.cloned.1.call-update) | async-done | bytes 2097168 | tf_op jit(solution)/shard_map/all_gather | solution.py:50
  162.8 6.8 convolution_convert_fusion.1
  169.7 1.9 reshape.70
  171.5 11.0 %all-gather.8.cloned.1.call-done = bf16[1536,512]{1,0:T(8,128)(2,1)} async-done(((bf16[384,512]{1,0:T(8,128)(2,1)}), bf16[1536,512]{1,0:T(8,128)(2,1)}) %all-gather.8.cloned.1.call-update) | async-done | bytes 1572880 | tf_op jit(solution)/shard_map/all_gather | solution.py:60
  182.5 3.1 fusion.13
  185.7 0.7 bitcast_select_fusion
  186.4 1.6 fusion.36
  188.0 1.8 convolution_bitcast_fusion
  189.8 4.2 convolution_bitcast_fusion.1
  194.0 2.1 pad_maximum_fusion
  196.1 0.0 reduce-scatter.8.cloned.1.call-update
  196.2 0.3 reduce-scatter.10.cloned.1.call-start
  196.4 1.1 copy-done.9
  197.5 3.8 fusion.10
  201.3 1.3 copy.27
  202.7 0.3 copy.43
  203.0 8.1 fusion.39
  211.1 0.0 reduce-scatter.10.cloned.1.call-update
  211.1 0.0 reduce-scatter.14.cloned.1.call-start
  211.2 1.3 copy-done.10
  212.5 3.9 fusion.9
  216.4 3.7 copy.23
  220.1 0.3 copy.42
  220.4 1.2 copy-done.3
  221.6 7.7 fusion.40
  229.3 0.0 reduce-scatter.14.cloned.1.call-update
  229.3 0.0 reduce-scatter.12.cloned.1.call-start
  229.4 4.4 reduce-scatter.8.cloned.1.call-done
  233.8 4.9 fusion.17
  238.7 0.0 reduce-scatter.6.cloned.1.call-start
  238.8 8.0 fusion.38
  246.8 0.3 all-gather.14.cloned.1.call-start
  247.1 0.1 dynamic-slice.3
  247.2 10.1 %fusion.37 = f32[1536,2048]{1,0:T(8,128)} fusion(bf16[1536,512]{1,0:T(8,128)(2,1)} %bitcast.80, bf16[512,2048]{1,0:T(8,128)(2,1)} %all-gather.12.cloned.1.call-done), kind=kOutput, calls=%fused_computation.59 | convolution fusion | flops 3221225472 | bytes 16252928 | tf_op jit(solution)/shard_map/dot_general | solution.py:63
  257.3 68.4 %reduce-scatter.10.cloned.1.call-done = f32[256,512]{1,0:T(8,128)} async-done(((f32[2048,512]{1,0:T(8,128)}), f32[256,512]{1,0:T(8,128)}) %reduce-scatter.10.cloned.1.call-update) | async-done | bytes 524304 | tf_op jit(solution)/shard_map/reduce_scatter | solution.py:74
  325.7 1.8 convert_element_type.65
  327.5 90.1 %reduce-scatter.14.cloned.1.call-done = f32[512,256]{1,0:T(8,128)} async-done(((f32[512,2048]{1,0:T(8,128)}), f32[512,256]{1,0:T(8,128)}) %reduce-scatter.14.cloned.1.call-update) | async-done | bytes 524304 | tf_op jit(solution)/shard_map/reduce_scatter | solution.py:67
  417.6 1.8 convert_element_type.67
  419.3 90.3 %reduce-scatter.12.cloned.1.call-done = f32[256,512]{1,0:T(8,128)} async-done(((f32[2048,512]{1,0:T(8,128)}), f32[256,512]{1,0:T(8,128)}) %reduce-scatter.12.cloned.1.call-update) | async-done | bytes 524304 | tf_op jit(solution)/shard_map/reduce_scatter | solution.py:76
  509.7 98.2 %reduce-scatter.6.cloned.1.call-done = f32[384,2048]{1,0:T(8,128)} async-done(((f32[1536,2048]{1,0:T(8,128)}), f32[384,2048]{1,0:T(8,128)}) %reduce-scatter.6.cloned.1.call-update) | async-done | bytes 3145744 | tf_op jit(solution)/shard_map/reduce_scatter | solution.py:71
  607.9 4.1 fusion.35
  612.0 3.6 multiply_convert_fusion.1
  615.6 1.0 copy-done.7
  616.6 258.6 %all-reduce.2 = (bf16[1536,2048]{1,0:T(8,128)(2,1)}, bf16[256,512]{1,0:T(8,128)(2,1)}) all-reduce(f32[1536,2048]{1,0:T(8,128)} %fusion.37, f32[256,512]{1,0:T(8,128)S(1)} %copy-done.7), channel_id=1, replica_groups=mesh['data'=8,'model'=4] {'model'}, use_global_device_ids=true, to_apply=%region_4.5 | all-reduce | flops 3276800 | bytes 19660800 | tf_op jit(solution)/shard_map/psum | solution.py:63
  875.3 6.6 copy.57
  (28 shorter events, 0.1 us)
Async XLA Ops:
  7.2 54.9 %all-gather.6.cloned.1.call-start = ((), (), s32[]{:S(2)}) async-start(), calls=%async_computation.5 | async-start | bytes 2359296 | tf_op jit(solution)/shard_map/all_gather | solution.py:51
  7.9 105.2 %all-gather.12.cloned.1.call-start = ((), (), s32[]{:S(2)}) async-start(), calls=%async_computation.8 | async-start | bytes 2359296 | tf_op jit(solution)/shard_map/all_gather | solution.py:52
  8.6 154.2 %all-gather.10.cloned.1.call-start = ((), (), s32[]{:S(2)}) async-start(), calls=%async_computation.7 | async-start | bytes 2359296 | tf_op jit(solution)/shard_map/all_gather | solution.py:50
  9.4 173.1 %all-gather.8.cloned.1.call-start = ((), (), s32[]{:S(2)}) async-start(), calls=%async_computation.6 | async-start | bytes 1966080 | tf_op jit(solution)/shard_map/all_gather | solution.py:60
  9.4 4.6 copy-start
  14.0 1.8 copy-start.11
  62.1 4.1 copy-start.12
  65.9 167.8 %reduce-scatter.8.cloned.1.call-start = ((), (), s32[]{:S(2)}) async-start(), calls=%async_computation.10 | async-start | bytes 3932160 | tf_op jit(solution)/shard_map/reduce_scatter | solution.py:70
  182.5 3.1 copy-start.5
  182.5 3.1 copy-start.8
  186.4 1.6 copy-start.4
  189.8 4.2 copy-start.6
  196.1 1.4 copy-start.9
  196.2 129.5 %reduce-scatter.10.cloned.1.call-start = ((), (), s32[]{:S(2)}) async-start(), calls=%async_computation.12 | async-start | bytes 4718592 | tf_op jit(solution)/shard_map/reduce_scatter | solution.py:74
  211.1 1.4 copy-start.10
  211.1 206.5 %reduce-scatter.14.cloned.1.call-start = ((), (), s32[]{:S(2)}) async-start(), calls=%async_computation.14 | async-start | bytes 4718592 | tf_op jit(solution)/shard_map/reduce_scatter | solution.py:67
  220.4 1.2 copy-start.3
  229.3 280.3 %reduce-scatter.12.cloned.1.call-start = ((), (), s32[]{:S(2)}) async-start(), calls=%async_computation.13 | async-start | bytes 4718592 | tf_op jit(solution)/shard_map/reduce_scatter | solution.py:76
  238.7 369.2 %reduce-scatter.6.cloned.1.call-start = ((), (), s32[]{:S(2)}) async-start(), calls=%async_computation.9 | async-start | bytes 15728640 | tf_op jit(solution)/shard_map/reduce_scatter | solution.py:71
  246.8 628.5 %all-gather.14.cloned.1.call-start = ((), (), s32[]{:S(2)}) async-start(), calls=%async_computation.11 | async-start | bytes 7864320 | tf_op jit(solution)/shard_map/all_gather | solution.py:83
  247.2 360.7 %copy-start.2 = (bf16[2048,512]{1,0:T(8,128)(2,1)S(1)}, bf16[2048,512]{1,0:T(8,128)(2,1)}, u32[]{:S(2)}) copy-start(bf16[2048,512]{1,0:T(8,128)(2,1)} %all-gather.6.cloned.1.call-done) | copy-start | bytes 6291460
  257.3 350.6 %copy-start.1 = (f32[384,512]{1,0:T(8,128)S(1)}, f32[384,512]{1,0:T(8,128)}, u32[]{:S(2)}) copy-start(f32[384,512]{1,0:T(8,128)} %reduce-scatter.8.cloned.1.call-done) | copy-start | bytes 2359300
  615.6 1.0 copy-start.7
Sparse Core Ops, SparseCore 0:
  10.1 51.9 all-gather.5
  64.1 48.9 all-gather.11
  115.3 47.4 all-gather.9
  164.2 18.2 all-gather.7
  196.3 37.4 reduce-scatter.7
  237.3 88.3 reduce-scatter.9
  329.3 88.1 reduce-scatter.13
  421.8 87.8 reduce-scatter.11
  512.3 95.5 reduce-scatter.5
  615.7 80.4 all-gather.13
where the time goes:
time: 889 us
  waiting for transfers between devices  493 us (55%)
  blocking collectives  259 us (29%)
  matrix products  78 us (9%)
  other arithmetic  23.9 us (3%)
  local copies, waits for them, and re-layouts  20.1 us (2%)
  between operations  14.3 us (2%)
    psum x1, blocking collectives, device_step(): lax.psum(jnp.dot(mixed, o_weight, preferred_element_type=jnp.float32), 'm...  259 us
    reduce_scatter x1, waiting for transfers between devices, device_step(): lax.psum_scatter(jnp.einsum('te,de->td', grad_query, q_weight, preferred_...  98.2 us
    reduce_scatter x1, waiting for transfers between devices, device_step(): lax.psum_scatter(grad_kv_w, 'data', scatter_dimension=0, tiled=True)  90.3 us
    reduce_scatter x1, waiting for transfers between devices, device_step(): lax.psum_scatter(grad_o_part, 'data', scatter_dimension=1, tiled=True)  90.1 us
    reduce_scatter x1, waiting for transfers between devices, device_step(): lax.psum_scatter(grad_q_part, 'data', scatter_dimension=0, tiled=True)  68.4 us
    all_gather x1, waiting for transfers between devices, device_step(): o_weight = lax.all_gather(o_weight_blk, 'data', axis=1, tiled=True)  46.9 us
    all_gather x1, waiting for transfers between devices, device_step(): q_weight = lax.all_gather(q_weight_blk, 'data', axis=0, tiled=True)  42.4 us
    all_gather x1, waiting for transfers between devices, device_step(): kv_weight = lax.all_gather(kv_weight_blk, 'data', axis=0, tiled=True)  38.9 us
  transfers between devices with their start and end apart: 10, of which 9 were waited for; matrix products, arithmetic and copies ran while one was open for 10% of the time, Pallas kernels for 0%

commit v1 on v0

v1 whole, which is shorter than its diff:
```python
import functools

import jax
import jax.numpy as jnp
from jax import lax
from jax.experimental import pallas as pl
from jax.experimental.pallas import tpu as pltpu
from jax.sharding import PartitionSpec as P

NORM_EPS = 1e-6
ROWS = 512
TOKS = 1536
SEQ = 128
BF = jnp.bfloat16
F32 = jnp.float32


def dot(a, b):
    return jnp.dot(a, b, preferred_element_type=F32)


def dot_t(a, b):
    return lax.dot_general(a, b, (((1,), (1,)), ((), ())), preferred_element_type=F32)


def t_dot(a, b):
    return lax.dot_general(a, b, (((0,), (0,)), ((), ())), preferred_element_type=F32)


MESH = pl.DeviceIdType.MESH


def cols(i, width=256):
    return pl.ds(pl.multiple_of(i * width, width), width)


def norm(x):
    c = x - jnp.mean(x, axis=-1, keepdims=True)
    inv = lax.rsqrt(jnp.mean(c * c, axis=-1, keepdims=True) + NORM_EPS)
    return c * inv, inv


def stack_heads(a):
    return jnp.concatenate([a[:, :256], a[:, 256:]], axis=0)


def spread_heads(a):
    return jnp.concatenate([a[:SEQ], a[SEQ:]], axis=1)


def softmax(s, mask2):
    s = jnp.where(mask2 > 0, s * (256 ** -0.5), -1e30)
    e = jnp.exp(s - jnp.max(s, axis=-1, keepdims=True))
    return e / jnp.sum(e, axis=-1, keepdims=True)


def attend(qs, ks, vs, mask2):
    scores = [dot_t(q, k) for q, k in zip(qs, ks)]
    probs = [softmax(s, mask2) for s in scores]
    return probs, [dot(p.astype(BF), v).astype(BF) for p, v in zip(probs, vs)]


def attend_back(qs, ks, vs, probs, dos):
    dps = [dot_t(do, v) for do, v in zip(dos, vs)]
    dvs = [t_dot(p.astype(BF), do) for p, do in zip(probs, dos)]
    dss = [p * (dp - jnp.sum(p * dp, axis=-1, keepdims=True)) for p, dp in zip(probs, dps)]
    dss = [(ds * (256 ** -0.5)).astype(BF) for ds in dss]
    dqs = [dot(ds, k).astype(BF) for ds, k in zip(dss, ks)]
    dks = [t_dot(ds, q) for ds, q in zip(dss, qs)]
    return dqs, dks, dvs


def drop(items, item):
    items[:] = [i for i in items if i is not item]


def layer_kernel(
    x_hbm, gain, wq_hbm, wkv_hbm, wo_hbm, dy_hbm, mask,
    y_out, dx_out, gq_out, gkv_out, go_out, wq_all, wo_all, o_all, dq_all, dkv_mate,
    xh, big, wq, wkv, wo, wqx, wox, q, k, v, probs, o, ox, dq, dqx, dkv,
    ofar, ory, orz, qfar, qry, qrz, kfar, kry, krz, acc, xt, stage, dkvt, go_st, gq_st, gk_st,
    lsem, ssem, rsem, gss, gsr, dks, dkr,
):
    d, m = lax.axis_index("data"), lax.axis_index("model")
    z, y = d // 2, d % 2
    core = m % 2
    zpeer = [((z + s) % 4) * 2 + y for s in range(4)]
    zfrom = [((z + 4 - s) % 4) * 2 + y for s in range(4)]
    yblk = [zfrom[s] + 1 - 2 * y for s in range(4)]
    ypeer = z * 2 + 1 - y
    mate = m + 1 - 2 * core
    across = (m + 2) % 4
    diag = (mate + 2) % 4
    mine = pl.ds(pl.multiple_of(core * 768, 768), 768)
    theirs = pl.ds(pl.multiple_of((1 - core) * 768, 768), 768)
    used = {"l": 0, "r": 0}
    sends = []

    def local(src, dst):
        i = used["l"]
        used["l"] += 1
        return pltpu.make_async_copy(src, dst, lsem.at[i])

    def remote(src, dst, land, axis, peer):
        i = used["r"]
        used["r"] += 1
        args = dict(send_sem=ssem.at[i], recv_sem=rsem.at[i], device_id={axis: peer}, device_id_type=MESH)
        out = pltpu.make_async_remote_copy(src_ref=src, dst_ref=dst, **args)
        back = pltpu.make_async_remote_copy(src_ref=land, dst_ref=land, **args)
        sends.append(out)
        return out, back

    loads = [local(x_hbm.at[cols(t, ROWS)], xh.at[cols(t, ROWS)]) for t in range(3)]
    half = cols(core)
    own = [local(wq_hbm, wq.at[cols(d)]), local(wkv_hbm.at[:, half], wkv.at[core, cols(d)]), local(wo_hbm, wo.at[:, cols(d)])]
    dy_load = local(dy_hbm, big.at[pl.ds(0, TOKS)])
    for c in loads + own + [dy_load]:
        c.start()

    barrier = pltpu.get_barrier_semaphore()
    for peer in zpeer[1:] + [ypeer]:
        pl.semaphore_signal(barrier, inc=1, device_id={"data": peer}, device_id_type=MESH)
    for peer in (mate, across, diag):
        pl.semaphore_signal(barrier, inc=1, device_id={"model": peer}, device_id_type=MESH)
    pl.semaphore_wait(barrier, 7)

    shard = [wq_hbm, wkv_hbm.at[:, half], wo_hbm]

    def slot(a, blk):
        return wq.at[cols(blk)] if a == 0 else wkv.at[core, cols(blk)] if a == 1 else wo.at[:, cols(blk)]

    def xslot(a, blk):
        return wqx.at[cols(blk)] if a == 0 else wox.at[:, cols(blk)]

    zs = {(a, s): remote(shard[a], slot(a, d), slot(a, zfrom[s]), "data", zpeer[s]) for a in range(3) for s in (1, 2, 3)}
    ys = {}
    xs = {}
    for a in range(3):
        for s in range(4):
            src = shard[a] if s == 0 else slot(a, zfrom[s])
            ys[a, s] = remote(src, slot(a, zfrom[s]), slot(a, yblk[s]), "data", ypeer)
            if a != 1:
                xs[a, s] = remote(src, xslot(a, zfrom[s]), xslot(a, zfrom[s]), "model", across)
                xs[a, 4 + s] = remote(slot(a, yblk[s]), xslot(a, yblk[s]), xslot(a, yblk[s]), "model", across)

    for s in (1, 2, 3):
        zs[0, s][0].start()
        zs[1, s][0].start()
    for a in range(3):
        ys[a, 0][0].start()
    for s in (1, 2, 3):
        zs[2, s][0].start()
    xs[0, 0][0].start()
    xs[2, 0][0].start()

    for t in range(3):
        loads[t].wait()

        @pl.loop(t * 4, t * 4 + 4)
        def _(i):
            r = cols(i, SEQ)
            n, _inv = norm(xh[r, :].astype(F32))
            xh[r, :] = (n * gain[...]).astype(BF)

    for c in own:
        c.wait()

    def forward(a, s):
        zs[a, s][1].wait_recv()
        ys[a, s][0].start()
        if a != 1:
            xs[a, s][0].start()

    def arrive(a, s):
        ys[a, s][1].wait_recv()
        if a != 1:
            xs[a, 4 + s][0].start()

    for s in (1, 2, 3):
        forward(0, s)
        forward(1, s)
    for s in (0, 1, 2):
        arrive(0, s)
        arrive(1, s)
    forward(2, 1)
    arrive(1, 3)
    kv_x = remote(wkv.at[core], wkv.at[core], wkv.at[1 - core], "model", mate)
    kv_x[0].start()
    arrive(0, 3)

    locals_ = []

    def share(src, dst, slot_of):
        c = local(src, dst.at[slot_of(0)])
        out, back = remote(src, dst.at[slot_of(0)], dst.at[slot_of(1)], "model", mate)
        c.start()
        out.start()
        locals_.append(c)
        return c, out, back

    def colslot(base):
        other = base + 1 - 2 * (base % 2)
        return lambda n: (slice(None), cols(base if n == 0 else other, 512))

    def rowslot(base):
        other = base + 1 - 2 * (base % 2)
        return lambda n: (cols(base if n == 0 else other, 512),)

    def share_rows(src, dst, base):
        other = base + 1 - 2 * (base % 2)
        c = local(src.at[mine], dst.at[:, cols(base, 512)])
        out, back = remote(src.at[theirs], dst.at[:, cols(base, 512)], dst.at[:, cols(other, 512)], "model", mate)
        c.start()
        out.start()
        locals_.append(c)
        return c, out, back

    wq_sh = share(wq, wq_all, colslot(m))

    @pl.loop(0, 3)
    def _(t):
        r = cols(t, ROWS)
        q[r, :] = dot(xh[r, :], wq[...]).astype(BF)

    forward(2, 2)
    kv_x[1].wait_recv()

    @pl.loop(0, 3)
    def _(t):
        r = cols(t, ROWS)
        k[r, :] = dot(xh[r, :], wkv[0]).astype(BF)
        v[r, :] = dot(xh[r, :], wkv[1]).astype(BF)

    forward(2, 3)
    mask2 = jnp.concatenate([mask[...], mask[...]], axis=0)

    @pl.loop(0, 3)
    def _(t):
        rows = [cols(t * 4 + b, SEQ) for b in range(4)]
        qs = [stack_heads(q[r, :]) for r in rows]
        ps, os = attend(qs, [k[r, :] for r in rows], [v[r, :] for r in rows], mask2)
        for b in range(4):
            probs[t * 4 + b] = ps[b]
            wide = spread_heads(os[b])
            o[rows[b], :] = wide
            big[pl.ds(TOKS, 512), rows[b]] = wide.T

    dy_load.wait()
    o_sh = share_rows(o, o_all, m)

    far = [qfar, kfar, ofar]
    ry = [qry, kry, ory]
    rz = [qrz, krz, orz]

    def piece(g, blk):
        if g == 2:
            return dot(big[pl.ds(TOKS, 512), pl.ds(0, TOKS)], big[pl.ds(0, TOKS), cols(blk)])
        return t_dot(xh[:, cols(blk)], dq[...] if g == 0 else q[:, cols(m, 128)])

    def ysend(g, kk):
        return pltpu.make_async_remote_copy(
            src_ref=far[g].at[kk], dst_ref=ry[g].at[kk], send_sem=gss.at[g, kk], recv_sem=gsr.at[g, kk],
            device_id={"data": ypeer}, device_id_type=MESH,
        )

    def zsend(g, kk):
        return pltpu.make_async_remote_copy(
            src_ref=ry[g].at[kk], dst_ref=rz[g].at[kk - 1], send_sem=gss.at[g, 4 + kk], recv_sem=gsr.at[g, 4 + kk],
            device_id={"data": zpeer[kk]}, device_id_type=MESH,
        )

    def send_far(g):
        @pl.loop(0, 4)
        def _(i):
            kk = (i + 1) % 4
            far[g][kk] = piece(g, ((z + kk) % 4) * 2 + 1 - y)
            ysend(g, kk).start()

    def near(g, kk):
        ysend(g, kk).wait_recv()
        ry[g][kk] = ry[g][kk] + piece(g, zpeer[kk])
        if kk:
            zsend(g, kk).start()

    def finish(g, st):
        for kk in (1, 2, 3):
            zsend(g, kk).wait_recv()
        st[...] = (ry[g][0] + rz[g][0] + rz[g][1] + rz[g][2]).astype(BF)

    send_far(2)
    for s in range(4):
        arrive(2, s)
    wo_sh = share(wo, wo_all, rowslot(m))

    def back_tile(t, q_of, ps, do, add):
        rows = [cols(t * 4 + b, SEQ) for b in range(4)]
        qs, ks, vs = q_of, [k[r, :] for r in rows], [v[r, :] for r in rows]
        dqs, dks, dvs = attend_back(qs, ks, vs, ps, [stack_heads(do[b * SEQ : (b + 1) * SEQ]) for b in range(4)])
        to = dqx if add else dq
        for b, r in enumerate(rows):
            to[r, :] = spread_heads(dqs[b])
            dkv[r, :256] = dkv[r, :256] + dks[b] if add else dks[b]
            dkv[r, 256:] = dkv[r, 256:] + dvs[b] if add else dvs[b]

    @pl.loop(0, 3)
    def _(t):
        do = dot_t(big[cols(t, ROWS), :], wo[...]).astype(BF)
        qs = [stack_heads(q[cols(t * 4 + b, SEQ), :]) for b in range(4)]
        back_tile(t, qs, [probs[t * 4 + b] for b in range(4)], do, False)

    dq_sh = share_rows(dq, dq_all, m)
    send_far(0)
    near(2, 1)
    near(2, 2)

    for n in range(8):
        xs[0, n][1].wait_recv()
        xs[2, n][1].wait_recv()
    wqx_sh = share(wqx, wq_all, colslot(across))
    wox_sh = share(wox, wo_all, rowslot(across))

    def dkv_send(t):
        r = cols(t, ROWS)
        return pltpu.make_async_remote_copy(
            src_ref=dkv.at[r], dst_ref=dkv_mate.at[r], send_sem=dks.at[t], recv_sem=dkr.at[t],
            device_id={"model": mate}, device_id_type=MESH,
        )

    @pl.loop(0, 3)
    def _(t):
        rows = [cols(t * 4 + b, SEQ) for b in range(4)]
        qm = dot(xh[cols(t, ROWS), :], wqx[...]).astype(BF)
        do = dot_t(big[cols(t, ROWS), :], wox[...]).astype(BF)
        qs = [stack_heads(qm[b * SEQ : (b + 1) * SEQ]) for b in range(4)]
        ps, os = attend(qs, [k[r, :] for r in rows], [v[r, :] for r in rows], mask2)
        for b in range(4):
            ox[rows[b], :] = spread_heads(os[b])
        back_tile(t, qs, ps, do, True)
        dkv_send(t).start()

    ox_sh = share_rows(ox, o_all, across)
    dqx_sh = share_rows(dqx, dq_all, across)
    near(2, 3)
    near(2, 0)

    tiles = []
    for t in range(3):
        dkv_send(t).wait_recv()
        tiles.append(local(dkv_mate.at[cols(t, ROWS)], dkvt.at[t % 2]))
        if t < 2:
            tiles[t].start()
    for t in range(3):
        tiles[t].wait()
        q[cols(t, ROWS), :] = (dkv[cols(t, ROWS), :] + dkvt[t % 2]).astype(BF)
        if t == 0:
            tiles[2].start()
    send_far(1)

    for sh in (wo_sh, wox_sh, o_sh, ox_sh):
        sh[0].wait()
        sh[1].wait_send()
        sh[2].wait_recv()
    for sh in (wo_sh, wox_sh, o_sh, ox_sh):
        drop(sends, sh[1])
        drop(locals_, sh[0])
    for c in [ys[2, s][0] for s in range(4)] + [xs[2, n][0] for n in range(8)]:
        c.wait_send()
        drop(sends, c)
    tin = [wox.at[pl.ds(0, 256)], wox.at[pl.ds(256, 256)], wo.at[pl.ds(0, 256)]]
    fill = local(wo_all, big)
    fill.start()
    ins = [local(o_all.at[cols(t)], tin[t]) for t in range(3)]
    for c in ins:
        c.start()
    near(0, 1)
    fill.wait()
    done = []

    def emit(t, dst):
        r = pl.ds(pl.multiple_of(core * 768 + t * 256, 256), 256)
        other = pl.ds(pl.multiple_of((1 - core) * 768 + t * 256, 256), 256)
        c = local(stage.at[t], dst.at[r])
        out, back = remote(stage.at[t], dst.at[r], dst.at[other], "model", mate)
        c.start()
        out.start()
        done.append((c, out, back))

    def tile_rows(t):
        return (wox, 256 * t) if t < 2 else (wo, 0)

    for t in range(3):
        ins[t].wait()
        ref, at = tile_rows(t)

        @pl.loop(0, 4)
        def _(i):
            stage[t, :, cols(i, 512)] = dot(ref[pl.ds(at, 256), :], big[:, cols(i, 512)]).astype(BF)

        emit(t, y_out)
        if t == 0:
            near(0, 2)

    for sh in (wq_sh, wqx_sh, dq_sh, dqx_sh):
        sh[0].wait()
        sh[1].wait_send()
        sh[2].wait_recv()
        drop(sends, sh[1])
        drop(locals_, sh[0])
    fill = local(wq_all, big)
    fill.start()
    ins = [local(dq_all.at[cols(t)], tin[t]) for t in range(3)]
    xin = [local(x_hbm.at[pl.ds(pl.multiple_of(core * 768 + t * 256, 256), 256)], xt.at[t % 2]) for t in range(3)]
    for c in ins + xin[:2]:
        c.start()
    near(0, 3)
    fill.wait()
    for t in range(3):
        ins[t].wait()
        ref, at = tile_rows(t)
        r = pl.ds(pl.multiple_of(core * 768 + t * 256, 256), 256)

        @pl.loop(0, 4)
        def _(i):
            c = cols(i, 512)
            g = dot_t(ref[pl.ds(at, 256), :], big[c, :])
            g = g + dot_t(q[r, :256], wkv[0, c, :])
            acc[:, c] = g + dot_t(q[r, 256:], wkv[1, c, :])

        xin[t].wait()
        done[t][0].wait()
        done[t][1].wait_send()
        drop(sends, done[t][1])

        @pl.loop(0, 2)
        def _(i):
            s = cols(i, SEQ)
            n, inv = norm(xt[t % 2, s, :].astype(F32))
            gn = acc[s, :] * gain[...]
            g = inv * (gn - jnp.mean(gn, axis=-1, keepdims=True) - n * jnp.mean(gn * n, axis=-1, keepdims=True))
            stage[t, s, :] = g.astype(BF)

        if t == 0:
            xin[2].start()
        emit(t, dx_out)
        if t == 0:
            near(0, 0)

    finish(2, go_st)
    fin = [local(go_st, go_out)]
    fin[0].start()
    for kk in (1, 2, 3, 0):
        near(1, kk)
    finish(0, gq_st)
    fin.append(local(gq_st, gq_out))
    fin[1].start()
    finish(1, gk_st)
    fin.append(local(gk_st, gkv_out.at[:, cols(m, 128)]))
    fin[2].start()
    backs = []
    for peer in (mate, across, diag):
        out, back = remote(gk_st, gkv_out.at[:, cols(m, 128)], gkv_out.at[:, cols(peer, 128)], "model", peer)
        out.start()
        backs.append(back)

    for b in backs:
        b.wait_recv()
    for t, (c, out, back) in enumerate(done):
        if t >= 3:
            c.wait()
        back.wait_recv()
    for c in sends:
        c.wait_send()
    for c in locals_ + fin:
        c.wait()
    for g in range(3):
        for kk in range(4):
            ysend(g, kk).wait_send()
            if kk:
                zsend(g, kk).wait_send()
    for t in range(3):
        dkv_send(t).wait_send()


def solution(mesh):
    sd = jax.ShapeDtypeStruct
    DMA = pltpu.SemaphoreType.DMA
    VM = pltpu.VMEM
    ANY = pl.BlockSpec(memory_space=pl.ANY)
    IN_VM = pl.BlockSpec(memory_space=pltpu.VMEM)

    def device_step(x, wq, wkv, wo, gain, positions, dy):
        mask = (positions[None, :] <= positions[:, None]).astype(F32)
        outs = [
            sd((TOKS, 2048), BF), sd((TOKS, 2048), BF), sd((256, 512), BF), sd((256, 512), BF), sd((512, 256), BF),
            sd((2048, 2048), BF), sd((2048, 2048), BF), sd((768, 2048), BF), sd((768, 2048), BF), sd((TOKS, 512), F32),
        ]
        wide, narrow = VM((TOKS, 512), BF), VM((TOKS, 256), BF)
        scratch = [
            VM((TOKS, 2048), BF), VM((2048, 2048), BF), VM((2048, 512), BF), VM((2, 2048, 256), BF), VM((512, 2048), BF),
            VM((2048, 512), BF), VM((512, 2048), BF), wide, narrow, narrow, VM((12, 256, SEQ), F32),
            wide, wide, wide, wide, VM((TOKS, 512), F32),
            VM((4, 512, 256), F32), VM((4, 512, 256), F32), VM((3, 512, 256), F32),
            VM((4, 256, 512), F32), VM((4, 256, 512), F32), VM((3, 256, 512), F32),
            VM((4, 256, 128), F32), VM((4, 256, 128), F32), VM((3, 256, 128), F32),
            VM((256, 2048), F32), VM((2, 256, 2048), BF), VM((3, 256, 2048), BF), VM((2, 512, 512), F32),
            VM((512, 256), BF), VM((256, 512), BF), VM((256, 128), BF),
            DMA((40,)), DMA((64,)), DMA((64,)), DMA((3, 8)), DMA((3, 8)), DMA((3,)), DMA((3,)),
        ]
        res = pl.pallas_call(
            layer_kernel,
            name="layer",
            in_specs=[ANY, IN_VM, ANY, ANY, ANY, ANY, IN_VM],
            out_specs=[ANY] * len(outs),
            out_shape=outs,
            scratch_shapes=scratch,
            cost_estimate=pl.CostEstimate(flops=80_000_000_000, bytes_accessed=100_000_000, transcendentals=0),
            compiler_params=pltpu.CompilerParams(collective_id=0, has_side_effects=True, vmem_limit_bytes=67043328),
        )(x, gain.reshape(1, -1), wq, wkv, wo, dy, mask)
        return tuple(res[:5])

    return jax.shard_map(
        device_step,
        mesh=mesh,
        in_specs=(P("data", None), P("data", "model"), P("data", None), P("model", "data"), P(), P(), P("data", None)),
        out_specs=(P("data", None), P("data", None), P("data", "model"), P("data", None), P("model", "data")),
        check_vma=False,
    )
```

time: 889 us -> 219 us (0.25)
  waiting for transfers between devices: 493 us -> 0 us
  blocking collectives: 259 us -> 0 us
  Pallas kernels: 0 us -> 205 us
  matrix products: 78 us -> 0 us
  other arithmetic: 23.9 us -> 1.44 us
  between operations: 14.3 us -> 0.66 us
    reduce_scatter x5 -> x0, waiting for transfers between devices: 351 us -> none  [the longest x1 98.2 us: device_step(): lax.psum_scatter(jnp.einsum('te,de->td', grad_query, q_weight, preferred_...]
    psum x1 -> x0, blocking collectives: 259 us -> none  [device_step(): lax.psum(jnp.dot(mixed, o_weight, preferred_element_type=jnp.float32), 'm...]
    pallas_call x0 -> x1, Pallas kernels: none -> 205 us  [device_step(): pl.pallas_call(layer_kernel, name='layer', in_specs=[ANY, IN_VM, ANY, ANY...]
    all_gather x5 -> x0, waiting for transfers between devices: 139 us -> none  [the longest x1 46.9 us: device_step(): o_weight = lax.all_gather(o_weight_blk, 'data', axis=1, tiled=True)]
    dot_general x15 -> x0, matrix products: 78 us -> none  [the longest x1 10.1 us: device_step(): jnp.dot(mixed, o_weight, preferred_element_type=jnp.float32)]
  transfers between devices with their start and end apart: 10 -> 0, of which waited for: 9 -> 0; matrix products, arithmetic and copies ran while one was open for 10% -> 0% of each run, Pallas kernels for 0% -> 0%
where the time goes in v1:
time: 219 us
  Pallas kernels  205 us (94%)
  local copies, waits for them, and re-layouts  11.6 us (5%)
    pallas_call x1, Pallas kernels, device_step(): pl.pallas_call(layer_kernel, name='layer', in_specs=[ANY, IN_VM, ANY, ANY...  205 us
    unnamed x13, local copies, waits for them, and re-layouts  11.6 us

profile of v1, /device:TPU:0, one launch (start us, length us, event | category | flops | bytes accessed | tf_op | source)
XLA Modules:
  0.0 218.5 jit_solution(9779606807498292890)
XLA Ops:
  0.6 1.4 compare_convert_fusion.mask
  2.1 204.9 %layer.1 = (bf16[1536,2048]{1,0:T(8,128)(2,1)}, bf16[1536,2048]{1,0:T(8,128)(2,1)}, bf16[256,512]{1,0:T(8,128)(2,1)}, bf16[256,512]{1,0:T(8,128)(2,1)}, bf16[512...) custom-call(bf16[1536,2048]{1,0:T(8,128)(2,1)} %x_hbm.1, ...), custom_call_target="tpu_custom_call" | custom-call | flops 80000000000 | bytes 100000000 | tf_op jit(solution)/shard_map/layer/pallas_call | solution.py:509
  206.9 0.0 copy-start
  206.9 6.8 %copy.17 = bf16[1536,2048]{1,0:T(8,128)(2,1)} copy(bf16[1536,2048]{1,0:T(8,128)(2,1)} %get-tuple-element.20) | data formatting | bytes 12582912
  213.7 0.0 copy-done
  213.7 0.0 copy-start.3
  213.7 0.0 copy-start.2
  213.7 0.0 copy-start.1
  213.7 2.7 %copy.18 = bf16[1536,2048]{1,0:T(8,128)(2,1)} copy(bf16[1536,2048]{1,0:T(8,128)(2,1)S(1)} %copy-done) | data formatting | bytes 12582912
  216.4 0.0 copy-done.3
  216.4 0.7 copy.19
  217.1 0.0 copy-done.2
  217.1 0.7 copy.20
  217.8 0.0 copy-done.1
  217.8 0.7 copy.21
Async XLA Ops:
  206.9 6.8 %copy-start = (bf16[1536,2048]{1,0:T(8,128)(2,1)S(1)}, bf16[1536,2048]{1,0:T(8,128)(2,1)}, u32[]{:S(2)}) copy-start(bf16[1536,2048]{1,0:T(8,128)(2,1)} %get-tuple-element.21) | copy-start | bytes 18874372
  213.7 2.7 %copy-start.3 = (bf16[256,512]{1,0:T(8,128)(2,1)S(1)}, bf16[256,512]{1,0:T(8,128)(2,1)}, u32[]{:S(2)}) copy-start(bf16[256,512]{1,0:T(8,128)(2,1)} %get-tuple-element.22) | copy-start | bytes 786436
  213.7 3.4 %copy-start.2 = (bf16[256,512]{1,0:T(8,128)(2,1)S(1)}, bf16[256,512]{1,0:T(8,128)(2,1)}, u32[]{:S(2)}) copy-start(bf16[256,512]{1,0:T(8,128)(2,1)} %get-tuple-element.23) | copy-start | bytes 786436
  213.7 4.1 %copy-start.1 = (bf16[512,256]{1,0:T(8,128)(2,1)S(1)}, bf16[512,256]{1,0:T(8,128)(2,1)}, u32[]{:S(2)}) copy-start(bf16[512,256]{1,0:T(8,128)(2,1)} %get-tuple-element.24) | copy-start | bytes 786436

commit v2 on v1

v2 whole, which is shorter than its diff:
```python
import functools

import jax
import jax.numpy as jnp
from jax import lax
from jax.experimental import pallas as pl
from jax.experimental.pallas import tpu as pltpu
from jax.sharding import PartitionSpec as P

NORM_EPS = 1e-6
ROWS = 512
TOKS = 1536
SEQ = 128
D = 2048
CORE = 768
W = 512
PASS = 384
H = 256
WAYS = (1, -1)
HOPS = (1, 2, 3)
BF = jnp.bfloat16
F32 = jnp.float32


def dot(a, b):
    return jnp.dot(a, b, preferred_element_type=F32)


def dot_t(a, b):
    return lax.dot_general(a, b, (((1,), (1,)), ((), ())), preferred_element_type=F32)


def t_dot(a, b):
    return lax.dot_general(a, b, (((0,), (0,)), ((), ())), preferred_element_type=F32)


MESH = pl.DeviceIdType.MESH


def cols(i, width=H):
    return pl.ds(pl.multiple_of(i * width, width), width)


def norm(x):
    c = x - jnp.mean(x, axis=-1, keepdims=True)
    inv = lax.rsqrt(jnp.mean(c * c, axis=-1, keepdims=True) + NORM_EPS)
    return c * inv, inv


def stack_heads(a):
    return jnp.concatenate([a[:, :H], a[:, H:]], axis=0)


def spread_heads(a):
    return jnp.concatenate([a[:SEQ], a[SEQ:]], axis=1)


def softmax(s, mask2):
    s = jnp.where(mask2 > 0, s * (H ** -0.5), -1e30)
    e = jnp.exp(s - jnp.max(s, axis=-1, keepdims=True))
    return e / jnp.sum(e, axis=-1, keepdims=True)


def attend(qs, ks, vs, mask2):
    scores = [dot_t(q, k) for q, k in zip(qs, ks)]
    probs = [softmax(s, mask2) for s in scores]
    return probs, [dot(p.astype(BF), v).astype(BF) for p, v in zip(probs, vs)]


def attend_back(qs, ks, vs, probs, dos):
    dps = [dot_t(do, v) for do, v in zip(dos, vs)]
    dvs = [t_dot(p.astype(BF), do) for p, do in zip(probs, dos)]
    dss = [p * (dp - jnp.sum(p * dp, axis=-1, keepdims=True)) for p, dp in zip(probs, dps)]
    dss = [(ds * (H ** -0.5)).astype(BF) for ds in dss]
    dqs = [dot(ds, k).astype(BF) for ds, k in zip(dss, ks)]
    dks = [t_dot(ds, q) for ds, q in zip(dss, qs)]
    return dqs, dks, dvs


def drop(items, item):
    items[:] = [i for i in items if i is not item]


def layer_kernel(
    x_hbm, gain, wq_hbm, wkv_hbm, wo_hbm, dy_hbm, pos,
    y_out, dx_out, gq_out, gkv_out, go_out, wq_all, wo_all, o_all, dq_all, dkv_mate,
    xh, big, wq, wkv, wo, wqx, wox, q, k, v, probs, o, ox, dq, dqx, dkv,
    ofar, ory, orz, qfar, qry, qrz, kfar, kry, krz, tin, stage, dkvt, go_st, gq_st, gk_st,
    lsem, ssem, rsem, gss, gsr, dks, dkr,
):
    d, m = lax.axis_index("data"), lax.axis_index("model")
    z, y = d // 2, d % 2
    core = m % 2
    zpeer = [((z + s) % 4) * 2 + y for s in range(4)]
    ypeer = z * 2 + 1 - y
    mate = m + 1 - 2 * core
    across = (m + 2) % 4
    diag = (mate + 2) % 4
    mine = pl.ds(pl.multiple_of(core * CORE, CORE), CORE)
    theirs = pl.ds(pl.multiple_of((1 - core) * CORE, CORE), CORE)
    used = {"l": 0, "r": 0}
    sends = []

    def local(src, dst):
        i = used["l"]
        used["l"] += 1
        return pltpu.make_async_copy(src, dst, lsem.at[i])

    def remote(src, dst, land, axis, peer, when=None):
        i = used["r"]
        used["r"] += 1
        args = dict(send_sem=ssem.at[i], recv_sem=rsem.at[i], device_id={axis: peer}, device_id_type=MESH)
        out = pltpu.make_async_remote_copy(src_ref=src, dst_ref=dst, **args)
        back = pltpu.make_async_remote_copy(src_ref=land, dst_ref=land, **args)
        sends.append((when, out))
        return out, back

    loads = [local(x_hbm.at[cols(t, ROWS)], xh.at[cols(t, ROWS)]) for t in range(3)]
    half = cols(core)
    own = [local(wq_hbm, wq.at[cols(d)]), local(wkv_hbm.at[:, half], wkv.at[core, cols(d)]), local(wo_hbm, wo.at[:, cols(d)])]
    dy_load = local(dy_hbm, big.at[pl.ds(0, TOKS)])
    for c in loads + own + [dy_load]:
        c.start()

    barrier = pltpu.get_barrier_semaphore()
    for peer in zpeer[1:] + [ypeer]:
        pl.semaphore_signal(barrier, inc=1, device_id={"data": peer}, device_id_type=MESH)
    for peer in (mate, across, diag):
        pl.semaphore_signal(barrier, inc=1, device_id={"model": peer}, device_id_type=MESH)
    pl.semaphore_wait(barrier, 7)

    shard = [wq_hbm, wkv_hbm.at[:, half], wo_hbm]

    def slot(a, zz):
        mineblk, otherblk = zz * 2 + y, zz * 2 + 1 - y
        return (
            wq.at[cols(mineblk)] if a == 0 else wkv.at[core, cols(mineblk)] if a == 1 else
            wo.at[:, cols(mineblk)] if a == 2 else wo.at[:, cols(otherblk)]
        )

    def other(a, zz):
        blk = zz * 2 + 1 - y
        return wq.at[cols(blk)] if a == 0 else wkv.at[core, cols(blk)] if a == 1 else wo.at[:, cols(blk)]

    def xslot(a, zz):
        blk = zz * 2 + (y if a in (0, 2) else 1 - y)
        return wqx.at[cols(blk)] if a in (0, 4) else wox.at[:, cols(blk)]

    def got(way, r):
        return z >= r if way > 0 else z + r <= 3

    def origin(way, r):
        return (z + 4 - r) % 4 if way > 0 else (z + r) % 4

    def goes(way):
        return z < 3 if way > 0 else z > 0

    def sent(way, r):
        return goes(way) if r == 1 else jnp.logical_and(got(way, r - 1), goes(way))

    hops, ys, xs = {}, {}, {}
    for r in HOPS:
        for way in WAYS:
            for a in range(4):
                here = origin(way, r - 1)
                src = shard[a] if r == 1 and a < 3 else slot(a, here)
                to = ((z + way + 4) % 4) * 2 + y
                hops[a, way, r] = remote(src, slot(a, here), slot(a, origin(way, r)), "data", to, sent(way, r))
    keys = [None] + [(way, r) for r in HOPS for way in WAYS]
    for key in keys:
        zz = z if key is None else origin(*key)
        cond = None if key is None else got(*key)
        for a in (0, 1):
            src = shard[a] if key is None else slot(a, zz)
            ys[a, key] = remote(src, slot(a, zz), other(a, zz), "data", ypeer, cond)
        if key is None:
            ys[2, None] = remote(shard[2], slot(2, z), slot(3, z), "data", ypeer)
        for a in (0, 2, 3, 4):
            src = shard[a] if key is None and a in (0, 2) else other(0, zz) if a == 4 else slot(a, zz)
            xs[a, key] = remote(src, xslot(a, zz), xslot(a, zz), "model", across, cond)

    def on(cond, fn):
        if cond is None:
            fn()
        else:
            pl.when(cond)(fn)

    def start_hop(a, way, r):
        on(sent(way, r), lambda: hops[a, way, r][0].start())

    for way in WAYS:
        for a in (0, 1):
            start_hop(a, way, 1)
    for a in (0, 1, 2):
        ys[a, None][0].start()
    xs[0, None][0].start()
    xs[2, None][0].start()

    for t in range(3):
        loads[t].wait()

        @pl.loop(t * 4, t * 4 + 4)
        def _(i):
            r = cols(i, SEQ)
            n, _inv = norm(xh[r, :].astype(F32))
            xh[r, :] = (n * gain[...]).astype(BF)

    for c in own:
        c.wait()

    for r in HOPS:
        for way in WAYS:

            @pl.when(got(way, r))
            def _():
                for a in (0, 1):
                    hops[a, way, r][1].wait_recv()
                    if r < 3:
                        start_hop(a, way, r + 1)
                    ys[a, (way, r)][0].start()
                xs[0, (way, r)][0].start()

        if r == 2:
            for way in WAYS:
                start_hop(2, way, 1)
            ys[2, None][1].wait_recv()
            for way in WAYS:
                start_hop(3, way, 1)
            xs[3, None][0].start()

    def take_wo(way, r):
        for a in (2, 3):
            hops[a, way, r][1].wait_recv()
            if r < 3:
                start_hop(a, way, r + 1)
            xs[a, (way, r)][0].start()

    def relay_wo(r):
        for way in WAYS:
            on(jnp.logical_and(got(way, r), goes(way)), lambda way=way: take_wo(way, r))

    def keep_wo():
        for r in HOPS:
            for way in WAYS:
                on(jnp.logical_and(got(way, r), jnp.logical_not(goes(way))), lambda way=way, r=r: take_wo(way, r))

    def arrive(key):
        def go():
            ys[0, key][1].wait_recv()
            ys[1, key][1].wait_recv()
            xs[4, key][0].start()

        on(None if key is None else got(*key), go)

    for key in keys[:5]:
        arrive(key)
    relay_wo(1)
    for key in keys[5:]:
        arrive(key)
    kv_x = remote(wkv.at[core], wkv.at[core], wkv.at[1 - core], "model", mate)
    kv_x[0].start()

    locals_ = []

    def share(src, dst, slot_of):
        c = local(src, dst.at[slot_of(0)])
        out, back = remote(src, dst.at[slot_of(0)], dst.at[slot_of(1)], "model", mate)
        c.start()
        out.start()
        locals_.append(c)
        return c, out, back

    def colslot(base):
        other = base + 1 - 2 * (base % 2)
        return lambda n: (slice(None), cols(base if n == 0 else other, W))

    def rowslot(base):
        other = base + 1 - 2 * (base % 2)
        return lambda n: (cols(base if n == 0 else other, W),)

    def share_rows(src, dst, base):
        other = base + 1 - 2 * (base % 2)
        c = local(src.at[mine], dst.at[:, cols(base, W)])
        out, back = remote(src.at[theirs], dst.at[:, cols(base, W)], dst.at[:, cols(other, W)], "model", mate)
        c.start()
        out.start()
        locals_.append(c)
        return c, out, back

    wq_sh = share(wq, wq_all, colslot(m))

    @pl.loop(0, 3)
    def _(t):
        r = cols(t, ROWS)
        q[r, :] = dot(xh[r, :], wq[...]).astype(BF)

    relay_wo(2)
    kv_x[1].wait_recv()

    @pl.loop(0, 3)
    def _(t):
        r = cols(t, ROWS)
        k[r, :] = dot(xh[r, :], wkv[0]).astype(BF)
        v[r, :] = dot(xh[r, :], wkv[1]).astype(BF)

    posm = jnp.broadcast_to(pos[...].astype(F32), (SEQ, SEQ))
    mask = (posm <= posm.T).astype(F32)
    mask2 = jnp.concatenate([mask, mask], axis=0)

    @pl.loop(0, 3)
    def _(t):
        rows = [cols(t * 4 + b, SEQ) for b in range(4)]
        qs = [stack_heads(q[r, :]) for r in rows]
        ps, os = attend(qs, [k[r, :] for r in rows], [v[r, :] for r in rows], mask2)
        for b in range(4):
            probs[t * 4 + b] = ps[b]
            wide = spread_heads(os[b])
            o[rows[b], :] = wide
            big[pl.ds(TOKS, W), rows[b]] = wide.T

    dy_load.wait()
    o_sh = share_rows(o, o_all, m)

    far = [qfar, kfar, ofar]
    ry = [qry, kry, ory]
    rz = [qrz, krz, orz]

    def piece(g, blk):
        if g == 2:
            return dot(big[pl.ds(TOKS, W), pl.ds(0, TOKS)], big[pl.ds(0, TOKS), cols(blk)])
        return t_dot(xh[:, cols(blk)], dq[...] if g == 0 else q[:, cols(m, SEQ)])

    def ysend(g, kk):
        return pltpu.make_async_remote_copy(
            src_ref=far[g].at[kk], dst_ref=ry[g].at[kk], send_sem=gss.at[g, kk], recv_sem=gsr.at[g, kk],
            device_id={"data": ypeer}, device_id_type=MESH,
        )

    def zsend(g, kk):
        return pltpu.make_async_remote_copy(
            src_ref=ry[g].at[kk], dst_ref=rz[g].at[kk - 1], send_sem=gss.at[g, 4 + kk], recv_sem=gsr.at[g, 4 + kk],
            device_id={"data": zpeer[kk]}, device_id_type=MESH,
        )

    def send_far(g, lo, hi):
        @pl.loop(lo, hi)
        def _(i):
            kk = 2 + i + (i // 2) * (1 - 2 * i)
            far[g][kk] = piece(g, ((z + kk) % 4) * 2 + 1 - y)
            ysend(g, kk).start()

    def near(g, kk):
        ysend(g, kk).wait_recv()
        ry[g][kk] = ry[g][kk] + piece(g, zpeer[kk])
        if kk:
            zsend(g, kk).start()

    def finish(g, st):
        for kk in HOPS:
            zsend(g, kk).wait_recv()
        st[...] = (ry[g][0] + rz[g][0] + rz[g][1] + rz[g][2]).astype(BF)

    send_far(2, 0, 4)
    relay_wo(3)
    keep_wo()
    wo_sh = share(wo, wo_all, rowslot(m))

    def back_tile(t, q_of, ps, do, add):
        rows = [cols(t * 4 + b, SEQ) for b in range(4)]
        qs, ks, vs = q_of, [k[r, :] for r in rows], [v[r, :] for r in rows]
        dqs, dks, dvs = attend_back(qs, ks, vs, ps, [stack_heads(do[b * SEQ : (b + 1) * SEQ]) for b in range(4)])
        to = dqx if add else dq
        for b, r in enumerate(rows):
            to[r, :] = spread_heads(dqs[b])
            dkv[r, :H] = dkv[r, :H] + dks[b] if add else dks[b]
            dkv[r, H:] = dkv[r, H:] + dvs[b] if add else dvs[b]

    @pl.loop(0, 3)
    def _(t):
        do = dot_t(big[cols(t, ROWS), :], wo[...]).astype(BF)
        qs = [stack_heads(q[cols(t * 4 + b, SEQ), :]) for b in range(4)]
        back_tile(t, qs, [probs[t * 4 + b] for b in range(4)], do, False)

    dq_sh = share_rows(dq, dq_all, m)
    send_far(0, 0, 2)
    near(2, 2)
    near(2, 3)
    near(2, 1)

    for key in keys:
        on(None if key is None else got(*key), lambda key=key: [xs[a, key][1].wait_recv() for a in (0, 2, 3, 4)] and None)
    wqx_sh = share(wqx, wq_all, colslot(across))
    wox_sh = share(wox, wo_all, rowslot(across))

    def dkv_send(t):
        r = cols(t, ROWS)
        return pltpu.make_async_remote_copy(
            src_ref=dkv.at[r], dst_ref=dkv_mate.at[r], send_sem=dks.at[t], recv_sem=dkr.at[t],
            device_id={"model": mate}, device_id_type=MESH,
        )

    @pl.loop(0, 3)
    def _(t):
        rows = [cols(t * 4 + b, SEQ) for b in range(4)]
        qm = dot(xh[cols(t, ROWS), :], wqx[...]).astype(BF)
        do = dot_t(big[cols(t, ROWS), :], wox[...]).astype(BF)
        qs = [stack_heads(qm[b * SEQ : (b + 1) * SEQ]) for b in range(4)]
        ps, os = attend(qs, [k[r, :] for r in rows], [v[r, :] for r in rows], mask2)
        for b in range(4):
            ox[rows[b], :] = spread_heads(os[b])
        back_tile(t, qs, ps, do, True)
        dkv_send(t).start()

    ox_sh = share_rows(ox, o_all, across)
    dqx_sh = share_rows(dqx, dq_all, across)

    tiles = []
    for t in range(3):
        dkv_send(t).wait_recv()
        tiles.append(local(dkv_mate.at[cols(t, ROWS)], dkvt.at[t % 2]))
        if t < 2:
            tiles[t].start()
    for t in range(3):
        tiles[t].wait()
        q[cols(t, ROWS), :] = (dkv[cols(t, ROWS), :] + dkvt[t % 2]).astype(BF)
        if t == 0:
            tiles[2].start()
    send_far(1, 0, 4)
    send_far(0, 2, 4)
    near(2, 0)

    for sh in (wo_sh, wox_sh, o_sh, ox_sh):
        sh[0].wait()
        sh[2].wait_recv()
        drop(locals_, sh[0])
    fill = local(wo_all, big)
    fill.start()
    fetch = local(o_all, tin)
    fetch.start()
    fill.wait()
    fetch.wait()

    def y_cols(lo, hi):
        @pl.loop(lo, hi)
        def _(i):
            stage[:, cols(i)] = dot(tin[...], big[:, cols(i)]).astype(BF)

    done = []

    def emit(dst):
        c = local(stage, dst.at[mine])
        out, back = remote(stage, dst.at[mine], dst.at[theirs], "model", mate)
        c.start()
        out.start()
        done.append((c, out, back))

    y_cols(0, 4)
    near(0, 2)
    y_cols(4, 8)
    emit(y_out)

    for sh in (wq_sh, wqx_sh, dq_sh, dqx_sh):
        sh[0].wait()
        sh[2].wait_recv()
        drop(locals_, sh[0])
    fill = local(wq_all, big)
    fill.start()
    fetch = local(dq_all, tin)
    fetch.start()
    wox_sh[1].wait_send()
    sends[:] = [s for s in sends if s[1] is not wox_sh[1]]
    xin = [local(x_hbm.at[pl.ds(pl.multiple_of(core * CORE + p * PASS, PASS), PASS)], wox.at[pl.ds(0, PASS)]) for p in range(2)]
    xin[0].start()
    for t in range(3):
        dkv_send(t).wait_send()
    near(0, 3)
    fill.wait()
    fetch.wait()
    for p in range(2):
        rows = pl.ds(pl.multiple_of(core * CORE + p * PASS, PASS), PASS)

        @pl.loop(0, 4)
        def _(i):
            c = cols(i, W)
            g = dot_t(tin[pl.ds(p * PASS, PASS), :], big[c, :])
            g = g + dot_t(q[rows, :H], wkv[0, c, :])
            dkv[cols(i, PASS), :] = g + dot_t(q[rows, H:], wkv[1, c, :])

        xin[p].wait()
        if p == 0:
            done[0][0].wait()
            done[0][1].wait_send()
            sends[:] = [s for s in sends if s[1] is not done[0][1]]

        @pl.loop(0, 3)
        def _(i):
            n, inv = norm(wox[cols(i, SEQ), :].astype(F32))
            gn = jnp.concatenate([dkv[pl.ds(pl.multiple_of(c * PASS + i * SEQ, SEQ), SEQ), :] for c in range(4)], axis=1) * gain[...]
            g = inv * (gn - jnp.mean(gn, axis=-1, keepdims=True) - n * jnp.mean(gn * n, axis=-1, keepdims=True))
            stage[pl.ds(pl.multiple_of(p * PASS + i * SEQ, SEQ), SEQ), :] = g.astype(BF)

        if p == 0:
            xin[1].start()
            for kk in (2, 3, 1, 0):
                near(1, kk)
    emit(dx_out)

    near(0, 1)
    finish(2, go_st)
    fin = [local(go_st, go_out)]
    fin[0].start()
    finish(1, gk_st)
    fin.append(local(gk_st, gkv_out.at[:, cols(m, SEQ)]))
    fin[1].start()
    backs = []
    for peer in (mate, across, diag):
        out, back = remote(gk_st, gkv_out.at[:, cols(m, SEQ)], gkv_out.at[:, cols(peer, SEQ)], "model", peer)
        out.start()
        backs.append(back)
    near(0, 0)
    finish(0, gq_st)
    fin.append(local(gq_st, gq_out))
    fin[2].start()

    for b in backs:
        b.wait_recv()
    done[1][0].wait()
    for c, out, back in done:
        back.wait_recv()
    for cond, c in sends:
        on(cond, c.wait_send)
    for c in locals_ + fin:
        c.wait()
    for g in range(3):
        for kk in range(4):
            ysend(g, kk).wait_send()
            if kk:
                zsend(g, kk).wait_send()


def copy_kernel(*refs):
    srcs, dsts, bufs, rsem, wsem = refs[:5], refs[5:10], refs[10:15], refs[15], refs[16]
    ins, outs = [], []
    for a in range(5):
        rows = srcs[a].shape[0]
        parts = 8 if a < 2 else 1
        for c in range(parts):
            r = pl.ds(c * (rows // parts), rows // parts)
            i = len(ins)
            ins.append(pltpu.make_async_copy(srcs[a].at[r], bufs[a].at[r], rsem.at[i]))
            outs.append(pltpu.make_async_copy(bufs[a].at[r], dsts[a].at[r], wsem.at[i]))
    for c in ins:
        c.start()
    for i, o in zip(ins, outs):
        i.wait()
        o.start()
    for o in outs:
        o.wait()


def solution(mesh):
    sd = jax.ShapeDtypeStruct
    DMA = pltpu.SemaphoreType.DMA
    VM = pltpu.VMEM
    ANY = pl.BlockSpec(memory_space=pl.ANY)
    IN_VM = pl.BlockSpec(memory_space=pltpu.VMEM)

    def device_step(x, wq, wkv, wo, gain, positions, dy):
        results = [
            sd((TOKS, D), BF), sd((TOKS, D), BF), sd((H, W), BF), sd((H, W), BF), sd((W, H), BF),
        ]
        outs = results + [
            sd((D, D), BF), sd((D, D), BF), sd((CORE, D), BF), sd((CORE, D), BF), sd((TOKS, W), F32),
        ]
        wide, narrow = VM((TOKS, W), BF), VM((TOKS, H), BF)
        scratch = [
            VM((TOKS, D), BF), VM((D, D), BF), VM((D, W), BF), VM((2, D, H), BF), VM((W, D), BF),
            VM((D, W), BF), VM((W, D), BF), wide, narrow, narrow, VM((12, H, SEQ), F32),
            wide, wide, wide, wide, VM((TOKS, W), F32),
            VM((4, W, H), F32), VM((4, W, H), F32), VM((3, W, H), F32),
            VM((4, H, W), F32), VM((4, H, W), F32), VM((3, H, W), F32),
            VM((4, H, SEQ), F32), VM((4, H, SEQ), F32), VM((3, H, SEQ), F32),
            VM((CORE, D), BF), VM((CORE, D), BF), VM((2, W, W), F32),
            VM((W, H), BF), VM((H, W), BF), VM((H, SEQ), BF),
            DMA((40,)), DMA((100,)), DMA((100,)), DMA((3, 8)), DMA((3, 8)), DMA((3,)), DMA((3,)),
        ]
        res = pl.pallas_call(
            layer_kernel,
            name="layer",
            in_specs=[ANY, IN_VM, ANY, ANY, ANY, ANY, IN_VM],
            out_specs=[ANY] * len(outs),
            out_shape=outs,
            scratch_shapes=scratch,
            cost_estimate=pl.CostEstimate(flops=80_000_000_000, bytes_accessed=100_000_000, transcendentals=0),
            compiler_params=pltpu.CompilerParams(collective_id=0, has_side_effects=True, vmem_limit_bytes=67043328),
        )(x, gain.reshape(1, -1), wq, wkv, wo, dy, positions.reshape(1, -1))
        return pl.pallas_call(
            copy_kernel,
            name="emit",
            in_specs=[ANY] * 5,
            out_specs=[ANY] * 5,
            out_shape=results,
            scratch_shapes=[VM(r.shape, r.dtype) for r in results] + [DMA((19,)), DMA((19,))],
            cost_estimate=pl.CostEstimate(flops=1_000_000, bytes_accessed=27_000_000, transcendentals=0),
            compiler_params=pltpu.CompilerParams(vmem_limit_bytes=60 * 2**20),
        )(*res[:5])

    return jax.shard_map(
        device_step,
        mesh=mesh,
        in_specs=(P("data", None), P("data", "model"), P("data", None), P("model", "data"), P(), P(), P("data", None)),
        out_specs=(P("data", None), P("data", None), P("data", "model"), P("data", None), P("model", "data")),
        check_vma=False,
    )
```

time: 219 us -> 199 us (0.909)
  local copies, waits for them, and re-layouts: 11.6 us -> 0 us
  Pallas kernels: 205 us -> 197 us
    pallas_call x1, Pallas kernels: 205 us -> 188 us  [device_step(): pl.pallas_call(layer_kernel, name='layer', in_specs=[ANY, IN_VM, ANY, ANY...]
    unnamed x13 -> x0, local copies, waits for them, and re-layouts: 11.6 us -> none
    pallas_call x0 -> x1, Pallas kernels: none -> 9.61 us  [device_step(): pl.pallas_call(copy_kernel, name='emit', in_specs=[ANY] * 5, out_specs=[A...]
where the time goes in v2:
time: 199 us; the launch traced here: 198 us
  Pallas kernels  197 us (99%)
    pallas_call x1, Pallas kernels, device_step(): pl.pallas_call(layer_kernel, name='layer', in_specs=[ANY, IN_VM, ANY, ANY...  188 us
    pallas_call x1, Pallas kernels, device_step(): pl.pallas_call(copy_kernel, name='emit', in_specs=[ANY] * 5, out_specs=[A...  9.61 us

profile of v2, /device:TPU:0, one launch (start us, length us, event | category | flops | bytes accessed | tf_op | source)
XLA Modules:
  0.0 198.0 jit_solution(5780519212185887059)
XLA Ops:
  0.6 187.5 %layer.1 = (bf16[1536,2048]{1,0:T(8,128)(2,1)}, bf16[1536,2048]{1,0:T(8,128)(2,1)}, bf16[256,512]{1,0:T(8,128)(2,1)}, bf16[256,512]{1,0:T(8,128)(2,1)}, bf16[512...) custom-call(bf16[1536,2048]{1,0:T(8,128)(2,1)} %x_hbm.1, ...), custom_call_target="tpu_custom_call" | custom-call | flops 80000000000 | bytes 100000000 | tf_op jit(solution)/shard_map/layer/pallas_call | solution.py:587
  188.2 9.6 %emit.1 = (bf16[1536,2048]{1,0:T(8,128)(2,1)}, bf16[1536,2048]{1,0:T(8,128)(2,1)}, bf16[256,512]{1,0:T(8,128)(2,1)}, bf16[256,512]{1,0:T(8,128)(2,1)}, bf16[512,256]{1,0:T(8,128)(2,1)}) custom-call(bf16[1536,2048]{1,0:T(8,128)(2,1)} %get-tuple-element.10.refs_0_, bf16[1536,2048]{1,0:T(8,128)(2,1)} %get-tuple-element.11.refs_1_, ...), custom_call_target="tpu_custom_call" | custom-call | flops 1000000 | bytes 27000000 | tf_op jit(solution)/shard_map/emit/pallas_call | solution.py:597

commit v3 on v2

--- a/solution.py
+++ b/solution.py
@@ -129,22 +129,11 @@
         pl.semaphore_signal(barrier, inc=1, device_id={"model": peer}, device_id_type=MESH)
     pl.semaphore_wait(barrier, 7)
 
-    shard = [wq_hbm, wkv_hbm.at[:, half], wo_hbm]
+    shard = {0: wq_hbm, 1: wkv_hbm.at[:, half], 3: wo_hbm}
 
     def slot(a, zz):
-        mineblk, otherblk = zz * 2 + y, zz * 2 + 1 - y
-        return (
-            wq.at[cols(mineblk)] if a == 0 else wkv.at[core, cols(mineblk)] if a == 1 else
-            wo.at[:, cols(mineblk)] if a == 2 else wo.at[:, cols(otherblk)]
-        )
-
-    def other(a, zz):
-        blk = zz * 2 + 1 - y
-        return wq.at[cols(blk)] if a == 0 else wkv.at[core, cols(blk)] if a == 1 else wo.at[:, cols(blk)]
-
-    def xslot(a, zz):
-        blk = zz * 2 + (y if a in (0, 2) else 1 - y)
-        return wqx.at[cols(blk)] if a in (0, 4) else wox.at[:, cols(blk)]
+        blk = zz * 2 + (1 - y if a in (2, 4) else y)
+        return wq.at[cols(blk)] if a == 0 else wkv.at[core, cols(blk)] if a < 3 else wo.at[:, cols(blk)]
 
     def got(way, r):
         return z >= r if way > 0 else z + r <= 3
@@ -158,26 +147,33 @@
     def sent(way, r):
         return goes(way) if r == 1 else jnp.logical_and(got(way, r - 1), goes(way))
 
-    hops, ys, xs = {}, {}, {}
+    hops, ys, xs, cs = {}, {}, {}, {}
     for r in HOPS:
         for way in WAYS:
-            for a in range(4):
+            for a in range(5):
                 here = origin(way, r - 1)
-                src = shard[a] if r == 1 and a < 3 else slot(a, here)
+                src = shard[a] if r == 1 and a in shard else slot(a, here)
                 to = ((z + way + 4) % 4) * 2 + y
                 hops[a, way, r] = remote(src, slot(a, here), slot(a, origin(way, r)), "data", to, sent(way, r))
     keys = [None] + [(way, r) for r in HOPS for way in WAYS]
+    for a in (1, 3):
+        ys[a, None] = remote(shard[a], slot(a, z), slot(a + 1, z), "data", ypeer)
     for key in keys:
         zz = z if key is None else origin(*key)
         cond = None if key is None else got(*key)
-        for a in (0, 1):
-            src = shard[a] if key is None else slot(a, zz)
-            ys[a, key] = remote(src, slot(a, zz), other(a, zz), "data", ypeer, cond)
-        if key is None:
-            ys[2, None] = remote(shard[2], slot(2, z), slot(3, z), "data", ypeer)
-        for a in (0, 2, 3, 4):
-            src = shard[a] if key is None and a in (0, 2) else other(0, zz) if a == 4 else slot(a, zz)
-            xs[a, key] = remote(src, xslot(a, zz), xslot(a, zz), "model", across, cond)
+        there = wq.at[cols(zz * 2 + 1 - y)]
+        src = wq_hbm if key is None else slot(0, zz)
+        ys[0, key] = remote(src, slot(0, zz), there, "data", ypeer, cond)
+        xs[0, key] = remote(src, wqx.at[cols(zz * 2 + y)], wqx.at[cols(zz * 2 + y)], "model", across, cond)
+        xs[5, key] = remote(there, wqx.at[cols(zz * 2 + 1 - y)], wqx.at[cols(zz * 2 + 1 - y)], "model", across, cond)
+        for a in (3, 4):
+            src = shard[a] if key is None and a == 3 else slot(a, zz)
+            to = wox.at[:, cols(zz * 2 + (y if a == 3 else 1 - y))]
+            xs[a, key] = remote(src, to, to, "model", across, cond)
+        for a in (1, 2):
+            src = shard[a] if key is None and a == 1 else slot(a, zz)
+            blk = zz * 2 + (y if a == 1 else 1 - y)
+            cs[a, key] = remote(src, slot(a, zz), wkv.at[1 - core, cols(blk)], "model", mate, cond)
 
     def on(cond, fn):
         if cond is None:
@@ -189,12 +185,12 @@
         on(sent(way, r), lambda: hops[a, way, r][0].start())
 
     for way in WAYS:
-        for a in (0, 1):
-            start_hop(a, way, 1)
-    for a in (0, 1, 2):
-        ys[a, None][0].start()
+        start_hop(0, way, 1)
+    ys[1, None][0].start()
+    ys[0, None][0].start()
     xs[0, None][0].start()
-    xs[2, None][0].start()
+    xs[3, None][0].start()
+    cs[1, None][0].start()
 
     for t in range(3):
         loads[t].wait()
@@ -208,57 +204,54 @@
     for c in own:
         c.wait()
 
-    for r in HOPS:
-        for way in WAYS:
-
-            @pl.when(got(way, r))
-            def _():
-                for a in (0, 1):
-                    hops[a, way, r][1].wait_recv()
-                    if r < 3:
-                        start_hop(a, way, r + 1)
-                    ys[a, (way, r)][0].start()
-                xs[0, (way, r)][0].start()
-
-        if r == 2:
-            for way in WAYS:
-                start_hop(2, way, 1)
-            ys[2, None][1].wait_recv()
-            for way in WAYS:
-                start_hop(3, way, 1)
-            xs[3, None][0].start()
-
-    def take_wo(way, r):
-        for a in (2, 3):
+    def take(arrays, way, r):
+        for a in arrays:
             hops[a, way, r][1].wait_recv()
             if r < 3:
                 start_hop(a, way, r + 1)
-            xs[a, (way, r)][0].start()
-
-    def relay_wo(r):
+            if a == 0:
+                ys[0, (way, r)][0].start()
+            if a in (1, 2):
+                cs[a, (way, r)][0].start()
+            else:
+                xs[a, (way, r)][0].start()
+
+    def relay(arrays, r):
         for way in WAYS:
-            on(jnp.logical_and(got(way, r), goes(way)), lambda way=way: take_wo(way, r))
-
-    def keep_wo():
-        for r in HOPS:
-            for way in WAYS:
-                on(jnp.logical_and(got(way, r), jnp.logical_not(goes(way))), lambda way=way, r=r: take_wo(way, r))
+            on(jnp.logical_and(got(way, r), goes(way)), lambda way=way: take(arrays, way, r))
+
+    def keep(arrays, r):
+        for way in WAYS:
+            on(jnp.logical_and(got(way, r), jnp.logical_not(goes(way))), lambda way=way: take(arrays, way, r))
+
+    def take_all(arrays, r):
+        for way in WAYS:
+            on(got(way, r), lambda way=way: take(arrays, way, r))
 
     def arrive(key):
         def go():
             ys[0, key][1].wait_recv()
-            ys[1, key][1].wait_recv()
-            xs[4, key][0].start()
+            xs[5, key][0].start()
 
         on(None if key is None else got(*key), go)
 
+    take_all((0,), 1)
+    take_all((0,), 2)
+    ys[1, None][1].wait_recv()
+    cs[2, None][0].start()
+    for way in WAYS:
+        for a in (1, 2):
+            start_hop(a, way, 1)
+    take_all((0,), 3)
+    ys[3, None][0].start()
+    take_all((1, 2), 1)
     for key in keys[:5]:
         arrive(key)
-    relay_wo(1)
+    relay((1, 2), 2)
+    for way in WAYS:
+        start_hop(3, way, 1)
     for key in keys[5:]:
         arrive(key)
-    kv_x = remote(wkv.at[core], wkv.at[core], wkv.at[1 - core], "model", mate)
-    kv_x[0].start()
 
     locals_ = []
 
@@ -294,8 +287,14 @@
         r = cols(t, ROWS)
         q[r, :] = dot(xh[r, :], wq[...]).astype(BF)
 
-    relay_wo(2)
-    kv_x[1].wait_recv()
+    ys[3, None][1].wait_recv()
+    xs[4, None][0].start()
+    for way in WAYS:
+        start_hop(4, way, 1)
+    keep((1, 2), 2)
+    take_all((1, 2), 3)
+    for key in keys:
+        on(None if key is None else got(*key), lambda key=key: [cs[a, key][1].wait_recv() for a in (1, 2)] and None)
 
     @pl.loop(0, 3)
     def _(t):
@@ -336,11 +335,27 @@
             device_id={"data": ypeer}, device_id_type=MESH,
         )
 
+    upper = z // 2
+    inner = jnp.logical_and(z > 0, z < 3)
+
+    def zcopy(g, kk, place, peer):
+        return pltpu.make_async_remote_copy(
+            src_ref=ry[g].at[kk], dst_ref=rz[g].at[place], send_sem=gss.at[g, 4 + kk], recv_sem=gsr.at[g, 4 + place],
+            device_id={"data": peer}, device_id_type=MESH,
+        )
+
     def zsend(g, kk):
-        return pltpu.make_async_remote_copy(
-            src_ref=ry[g].at[kk], dst_ref=rz[g].at[kk - 1], send_sem=gss.at[g, 4 + kk], recv_sem=gsr.at[g, 4 + kk],
-            device_id={"data": zpeer[kk]}, device_id_type=MESH,
-        )
+        if kk == 2:
+            return zcopy(g, kk, 2 + upper, (z + 1 - 2 * upper) * 2 + y)
+        return zcopy(g, kk, kk // 2, zpeer[kk])
+
+    def merge(g):
+        @pl.when(inner)
+        def _():
+            for kk in (3, 1):
+                zcopy(g, 2, 2 + kk // 2, ypeer).wait_recv()
+                ry[g][kk] = ry[g][kk] + rz[g][2 + kk // 2]
+                zsend(g, kk).start()
 
     def send_far(g, lo, hi):
         @pl.loop(lo, hi)
@@ -352,17 +367,23 @@
     def near(g, kk):
         ysend(g, kk).wait_recv()
         ry[g][kk] = ry[g][kk] + piece(g, zpeer[kk])
-        if kk:
+        if kk == 2:
             zsend(g, kk).start()
+        elif kk:
+            pl.when(jnp.logical_not(inner))(lambda: zsend(g, kk).start())
 
     def finish(g, st):
-        for kk in HOPS:
+        for kk in (1, 3):
             zsend(g, kk).wait_recv()
-        st[...] = (ry[g][0] + rz[g][0] + rz[g][1] + rz[g][2]).astype(BF)
+        st[...] = (ry[g][0] + rz[g][0] + rz[g][1]).astype(BF)
 
     send_far(2, 0, 4)
-    relay_wo(3)
-    keep_wo()
+    relay((3, 4), 1)
+    relay((3, 4), 2)
+    near(2, 2)
+    keep((3, 4), 1)
+    keep((3, 4), 2)
+    take_all((3, 4), 3)
     wo_sh = share(wo, wo_all, rowslot(m))
 
     def back_tile(t, q_of, ps, do, add):
@@ -382,13 +403,13 @@
         back_tile(t, qs, [probs[t * 4 + b] for b in range(4)], do, False)
 
     dq_sh = share_rows(dq, dq_all, m)
-    send_far(0, 0, 2)
-    near(2, 2)
+    send_far(0, 0, 4)
     near(2, 3)
     near(2, 1)
+    merge(2)
 
     for key in keys:
-        on(None if key is None else got(*key), lambda key=key: [xs[a, key][1].wait_recv() for a in (0, 2, 3, 4)] and None)
+        on(None if key is None else got(*key), lambda key=key: [xs[a, key][1].wait_recv() for a in (0, 3, 4, 5)] and None)
     wqx_sh = share(wqx, wq_all, colslot(across))
     wox_sh = share(wox, wo_all, rowslot(across))
 
@@ -426,18 +447,18 @@
         if t == 0:
             tiles[2].start()
     send_far(1, 0, 4)
-    send_far(0, 2, 4)
     near(2, 0)
+    near(0, 2)
 
     for sh in (wo_sh, wox_sh, o_sh, ox_sh):
         sh[0].wait()
         sh[2].wait_recv()
         drop(locals_, sh[0])
-    fill = local(wo_all, big)
-    fill.start()
     fetch = local(o_all, tin)
     fetch.start()
-    fill.wait()
+    fill = [local(wo_all.at[:, cols(i, W)], big.at[:, cols(i, W)]) for i in range(4)]
+    for c in fill:
+        c.start()
     fetch.wait()
 
     def y_cols(lo, hi):
@@ -454,37 +475,46 @@
         out.start()
         done.append((c, out, back))
 
-    y_cols(0, 4)
-    near(0, 2)
-    y_cols(4, 8)
+    for i in range(4):
+        fill[i].wait()
+        y_cols(2 * i, 2 * i + 2)
+        if i == 1:
+            near(0, 3)
     emit(y_out)
 
     for sh in (wq_sh, wqx_sh, dq_sh, dqx_sh):
         sh[0].wait()
         sh[2].wait_recv()
         drop(locals_, sh[0])
-    fill = local(wq_all, big)
-    fill.start()
     fetch = local(dq_all, tin)
     fetch.start()
+    fill = [local(wq_all.at[cols(i, W)], big.at[cols(i, W)]) for i in range(4)]
+    for c in fill:
+        c.start()
     wox_sh[1].wait_send()
     sends[:] = [s for s in sends if s[1] is not wox_sh[1]]
     xin = [local(x_hbm.at[pl.ds(pl.multiple_of(core * CORE + p * PASS, PASS), PASS)], wox.at[pl.ds(0, PASS)]) for p in range(2)]
     xin[0].start()
     for t in range(3):
         dkv_send(t).wait_send()
-    near(0, 3)
-    fill.wait()
+    near(0, 1)
+    merge(0)
     fetch.wait()
     for p in range(2):
         rows = pl.ds(pl.multiple_of(core * CORE + p * PASS, PASS), PASS)
 
-        @pl.loop(0, 4)
-        def _(i):
+        def dh_cols(i):
             c = cols(i, W)
             g = dot_t(tin[pl.ds(p * PASS, PASS), :], big[c, :])
             g = g + dot_t(q[rows, :H], wkv[0, c, :])
             dkv[cols(i, PASS), :] = g + dot_t(q[rows, H:], wkv[1, c, :])
+
+        if p == 0:
+            for n in range(4):
+                fill[n].wait()
+                pl.loop(n, n + 1)(dh_cols)
+        else:
+            pl.loop(0, 4)(dh_cols)
 
         xin[p].wait()
         if p == 0:
@@ -501,26 +531,27 @@
 
         if p == 0:
             xin[1].start()
-            for kk in (2, 3, 1, 0):
-                near(1, kk)
+            near(0, 0)
     emit(dx_out)
 
-    near(0, 1)
+    for kk in (2, 3, 1):
+        near(1, kk)
+    merge(1)
+    near(1, 0)
     finish(2, go_st)
     fin = [local(go_st, go_out)]
     fin[0].start()
+    finish(0, gq_st)
+    fin.append(local(gq_st, gq_out))
+    fin[1].start()
     finish(1, gk_st)
     fin.append(local(gk_st, gkv_out.at[:, cols(m, SEQ)]))
-    fin[1].start()
+    fin[2].start()
     backs = []
     for peer in (mate, across, diag):
         out, back = remote(gk_st, gkv_out.at[:, cols(m, SEQ)], gkv_out.at[:, cols(peer, SEQ)], "model", peer)
         out.start()
         backs.append(back)
-    near(0, 0)
-    finish(0, gq_st)
-    fin.append(local(gq_st, gq_out))
-    fin[2].start()
 
     for b in backs:
         b.wait_recv()
@@ -577,12 +608,12 @@
             VM((TOKS, D), BF), VM((D, D), BF), VM((D, W), BF), VM((2, D, H), BF), VM((W, D), BF),
             VM((D, W), BF), VM((W, D), BF), wide, narrow, narrow, VM((12, H, SEQ), F32),
             wide, wide, wide, wide, VM((TOKS, W), F32),
-            VM((4, W, H), F32), VM((4, W, H), F32), VM((3, W, H), F32),
-            VM((4, H, W), F32), VM((4, H, W), F32), VM((3, H, W), F32),
-            VM((4, H, SEQ), F32), VM((4, H, SEQ), F32), VM((3, H, SEQ), F32),
+            VM((4, W, H), F32), VM((4, W, H), F32), VM((4, W, H), F32),
+            VM((4, H, W), F32), VM((4, H, W), F32), VM((4, H, W), F32),
+            VM((4, H, SEQ), F32), VM((4, H, SEQ), F32), VM((4, H, SEQ), F32),
             VM((CORE, D), BF), VM((CORE, D), BF), VM((2, W, W), F32),
             VM((W, H), BF), VM((H, W), BF), VM((H, SEQ), BF),
-            DMA((40,)), DMA((100,)), DMA((100,)), DMA((3, 8)), DMA((3, 8)), DMA((3,)), DMA((3,)),
+            DMA((48,)), DMA((112,)), DMA((112,)), DMA((3, 8)), DMA((3, 8)), DMA((3,)), DMA((3,)),
         ]
         res = pl.pallas_call(
             layer_kernel,

time: 199 us -> 182 us (0.915)
  Pallas kernels: 197 us -> 181 us
    pallas_call x1, Pallas kernels: 188 us -> 171 us  [device_step(): pl.pallas_call(layer_kernel, name='layer', in_specs=[ANY, IN_VM, ANY, ANY...]
where the time goes in v3:
time: 182 us
  Pallas kernels  181 us (99%)
    pallas_call x1, Pallas kernels, device_step(): pl.pallas_call(layer_kernel, name='layer', in_specs=[ANY, IN_VM, ANY, ANY...  171 us
    pallas_call x1, Pallas kernels, device_step(): pl.pallas_call(copy_kernel, name='emit', in_specs=[ANY] * 5, out_specs=[A...  9.61 us

profile of v3, /device:TPU:0, one launch (start us, length us, event | category | flops | bytes accessed | tf_op | source)
XLA Modules:
  0.0 181.9 jit_solution(17664647423880458711)
XLA Ops:
  0.6 171.5 %layer.1 = (bf16[1536,2048]{1,0:T(8,128)(2,1)}, bf16[1536,2048]{1,0:T(8,128)(2,1)}, bf16[256,512]{1,0:T(8,128)(2,1)}, bf16[256,512]{1,0:T(8,128)(2,1)}, bf16[512...) custom-call(bf16[1536,2048]{1,0:T(8,128)(2,1)} %x_hbm.1, ...), custom_call_target="tpu_custom_call" | custom-call | flops 80000000000 | bytes 100000000 | tf_op jit(solution)/shard_map/layer/pallas_call | solution.py:618
  172.1 9.6 %emit.1 = (bf16[1536,2048]{1,0:T(8,128)(2,1)}, bf16[1536,2048]{1,0:T(8,128)(2,1)}, bf16[256,512]{1,0:T(8,128)(2,1)}, bf16[256,512]{1,0:T(8,128)(2,1)}, bf16[512,256]{1,0:T(8,128)(2,1)}) custom-call(bf16[1536,2048]{1,0:T(8,128)(2,1)} %get-tuple-element.10.refs_0_, bf16[1536,2048]{1,0:T(8,128)(2,1)} %get-tuple-element.11.refs_1_, ...), custom_call_target="tpu_custom_call" | custom-call | flops 1000000 | bytes 27000000 | tf_op jit(solution)/shard_map/emit/pallas_call | solution.py:628

commit v4 on v3

--- a/solution.py
+++ b/solution.py
@@ -150,14 +150,13 @@
     hops, ys, xs, cs = {}, {}, {}, {}
     for r in HOPS:
         for way in WAYS:
-            for a in range(5):
+            for a in (0, 1, 3, 4):
                 here = origin(way, r - 1)
                 src = shard[a] if r == 1 and a in shard else slot(a, here)
                 to = ((z + way + 4) % 4) * 2 + y
                 hops[a, way, r] = remote(src, slot(a, here), slot(a, origin(way, r)), "data", to, sent(way, r))
     keys = [None] + [(way, r) for r in HOPS for way in WAYS]
-    for a in (1, 3):
-        ys[a, None] = remote(shard[a], slot(a, z), slot(a + 1, z), "data", ypeer)
+    ys[3, None] = remote(wo_hbm, slot(3, z), slot(4, z), "data", ypeer)
     for key in keys:
         zz = z if key is None else origin(*key)
         cond = None if key is None else got(*key)
@@ -170,10 +169,11 @@
             src = shard[a] if key is None and a == 3 else slot(a, zz)
             to = wox.at[:, cols(zz * 2 + (y if a == 3 else 1 - y))]
             xs[a, key] = remote(src, to, to, "model", across, cond)
+        src = shard[1] if key is None else slot(1, zz)
+        ys[1, key] = remote(src, slot(1, zz), slot(2, zz), "data", ypeer, cond)
         for a in (1, 2):
-            src = shard[a] if key is None and a == 1 else slot(a, zz)
             blk = zz * 2 + (y if a == 1 else 1 - y)
-            cs[a, key] = remote(src, slot(a, zz), wkv.at[1 - core, cols(blk)], "model", mate, cond)
+            cs[a, key] = remote(src if a == 1 else slot(2, zz), slot(a, zz), wkv.at[1 - core, cols(blk)], "model", mate, cond)
 
     def on(cond, fn):
         if cond is None:
@@ -186,8 +186,8 @@
 
     for way in WAYS:
         start_hop(0, way, 1)
+    ys[0, None][0].start()
     ys[1, None][0].start()
-    ys[0, None][0].start()
     xs[0, None][0].start()
     xs[3, None][0].start()
     cs[1, None][0].start()
@@ -209,12 +209,9 @@
             hops[a, way, r][1].wait_recv()
             if r < 3:
                 start_hop(a, way, r + 1)
-            if a == 0:
-                ys[0, (way, r)][0].start()
-            if a in (1, 2):
-                cs[a, (way, r)][0].start()
-            else:
-                xs[a, (way, r)][0].start()
+            if a < 2:
+                ys[a, (way, r)][0].start()
+            (cs if a == 1 else xs)[a, (way, r)][0].start()
 
     def relay(arrays, r):
         for way in WAYS:
@@ -228,30 +225,26 @@
         for way in WAYS:
             on(got(way, r), lambda way=way: take(arrays, way, r))
 
-    def arrive(key):
+    def arrive(a, key):
         def go():
-            ys[0, key][1].wait_recv()
-            xs[5, key][0].start()
+            ys[a, key][1].wait_recv()
+            (cs[2, key] if a else xs[5, key])[0].start()
 
         on(None if key is None else got(*key), go)
 
     take_all((0,), 1)
     take_all((0,), 2)
-    ys[1, None][1].wait_recv()
-    cs[2, None][0].start()
     for way in WAYS:
-        for a in (1, 2):
-            start_hop(a, way, 1)
+        start_hop(1, way, 1)
     take_all((0,), 3)
-    ys[3, None][0].start()
-    take_all((1, 2), 1)
+    take_all((1,), 1)
     for key in keys[:5]:
-        arrive(key)
-    relay((1, 2), 2)
+        arrive(0, key)
+    relay((1,), 2)
     for way in WAYS:
         start_hop(3, way, 1)
     for key in keys[5:]:
-        arrive(key)
+        arrive(0, key)
 
     locals_ = []
 
@@ -287,12 +280,11 @@
         r = cols(t, ROWS)
         q[r, :] = dot(xh[r, :], wq[...]).astype(BF)
 
-    ys[3, None][1].wait_recv()
-    xs[4, None][0].start()
-    for way in WAYS:
-        start_hop(4, way, 1)
-    keep((1, 2), 2)
-    take_all((1, 2), 3)
+    keep((1,), 2)
+    take_all((1,), 3)
+    ys[3, None][0].start()
+    for key in keys:
+        arrive(1, key)
     for key in keys:
         on(None if key is None else got(*key), lambda key=key: [cs[a, key][1].wait_recv() for a in (1, 2)] and None)
 
@@ -302,6 +294,10 @@
         k[r, :] = dot(xh[r, :], wkv[0]).astype(BF)
         v[r, :] = dot(xh[r, :], wkv[1]).astype(BF)
 
+    ys[3, None][1].wait_recv()
+    xs[4, None][0].start()
+    for way in WAYS:
+        start_hop(4, way, 1)
     posm = jnp.broadcast_to(pos[...].astype(F32), (SEQ, SEQ))
     mask = (posm <= posm.T).astype(F32)
     mask2 = jnp.concatenate([mask, mask], axis=0)
@@ -345,8 +341,10 @@
         )
 
     def zsend(g, kk):
+        if kk == 2 and g != 1:
+            return zcopy(g, kk, 2 + upper, (z + 1 - 2 * upper) * 2 + y)
         if kk == 2:
-            return zcopy(g, kk, 2 + upper, (z + 1 - 2 * upper) * 2 + y)
+            return zcopy(g, kk, 2, zpeer[2])
         return zcopy(g, kk, kk // 2, zpeer[kk])
 
     def merge(g):
@@ -367,7 +365,7 @@
     def near(g, kk):
         ysend(g, kk).wait_recv()
         ry[g][kk] = ry[g][kk] + piece(g, zpeer[kk])
-        if kk == 2:
+        if kk == 2 or kk and g == 1:
             zsend(g, kk).start()
         elif kk:
             pl.when(jnp.logical_not(inner))(lambda: zsend(g, kk).start())
@@ -375,7 +373,11 @@
     def finish(g, st):
         for kk in (1, 3):
             zsend(g, kk).wait_recv()
-        st[...] = (ry[g][0] + rz[g][0] + rz[g][1]).astype(BF)
+        total = ry[g][0] + rz[g][0] + rz[g][1]
+        if g == 1:
+            zsend(g, 2).wait_recv()
+            total = total + rz[g][2]
+        st[...] = total.astype(BF)
 
     send_far(2, 0, 4)
     relay((3, 4), 1)
@@ -403,14 +405,29 @@
         back_tile(t, qs, [probs[t * 4 + b] for b in range(4)], do, False)
 
     dq_sh = share_rows(dq, dq_all, m)
-    send_far(0, 0, 4)
+    send_far(0, 0, 3)
     near(2, 3)
     near(2, 1)
     merge(2)
 
     for key in keys:
-        on(None if key is None else got(*key), lambda key=key: [xs[a, key][1].wait_recv() for a in (0, 3, 4, 5)] and None)
+        on(None if key is None else got(*key), lambda key=key: [xs[a, key][1].wait_recv() for a in (0, 5)] and None)
     wqx_sh = share(wqx, wq_all, colslot(across))
+
+    @pl.loop(0, 3)
+    def _(t):
+        rows = [cols(t * 4 + b, SEQ) for b in range(4)]
+        qm = dot(xh[cols(t, ROWS), :], wqx[...]).astype(BF)
+        qs = [stack_heads(qm[b * SEQ : (b + 1) * SEQ]) for b in range(4)]
+        ps, os = attend(qs, [k[r, :] for r in rows], [v[r, :] for r in rows], mask2)
+        dqx[cols(t, ROWS), :] = qm
+        for b in range(4):
+            probs[t * 4 + b] = ps[b]
+            ox[rows[b], :] = spread_heads(os[b])
+
+    ox_sh = share_rows(ox, o_all, across)
+    for key in keys:
+        on(None if key is None else got(*key), lambda key=key: [xs[a, key][1].wait_recv() for a in (3, 4)] and None)
     wox_sh = share(wox, wo_all, rowslot(across))
 
     def dkv_send(t):
@@ -422,17 +439,11 @@
 
     @pl.loop(0, 3)
     def _(t):
-        rows = [cols(t * 4 + b, SEQ) for b in range(4)]
-        qm = dot(xh[cols(t, ROWS), :], wqx[...]).astype(BF)
         do = dot_t(big[cols(t, ROWS), :], wox[...]).astype(BF)
-        qs = [stack_heads(qm[b * SEQ : (b + 1) * SEQ]) for b in range(4)]
-        ps, os = attend(qs, [k[r, :] for r in rows], [v[r, :] for r in rows], mask2)
-        for b in range(4):
-            ox[rows[b], :] = spread_heads(os[b])
-        back_tile(t, qs, ps, do, True)
+        qs = [stack_heads(dqx[cols(t * 4 + b, SEQ), :]) for b in range(4)]
+        back_tile(t, qs, [probs[t * 4 + b] for b in range(4)], do, True)
         dkv_send(t).start()
 
-    ox_sh = share_rows(ox, o_all, across)
     dqx_sh = share_rows(dqx, dq_all, across)
 
     tiles = []
@@ -447,6 +458,7 @@
         if t == 0:
             tiles[2].start()
     send_far(1, 0, 4)
+    send_far(0, 3, 4)
     near(2, 0)
     near(0, 2)
 
@@ -531,28 +543,26 @@
 
         if p == 0:
             xin[1].start()
-            near(0, 0)
+            for kk in (2, 3, 1, 0):
+                near(1, kk)
     emit(dx_out)
 
-    for kk in (2, 3, 1):
-        near(1, kk)
-    merge(1)
-    near(1, 0)
     finish(2, go_st)
     fin = [local(go_st, go_out)]
     fin[0].start()
-    finish(0, gq_st)
-    fin.append(local(gq_st, gq_out))
-    fin[1].start()
     finish(1, gk_st)
     fin.append(local(gk_st, gkv_out.at[:, cols(m, SEQ)]))
-    fin[2].start()
+    fin[1].start()
     backs = []
     for peer in (mate, across, diag):
         out, back = remote(gk_st, gkv_out.at[:, cols(m, SEQ)], gkv_out.at[:, cols(peer, SEQ)], "model", peer)
         out.start()
         backs.append(back)
 
+    near(0, 0)
+    finish(0, gq_st)
+    fin.append(local(gq_st, gq_out))
+    fin[2].start()
     for b in backs:
         b.wait_recv()
     done[1][0].wait()

time: 182 us -> 182 us (level)
  no operation moved by 1% of the time
where the time goes in v4:
time: 182 us
  Pallas kernels  181 us (99%)
    pallas_call x1, Pallas kernels, device_step(): pl.pallas_call(layer_kernel, name='layer', in_specs=[ANY, IN_VM, ANY, ANY...  171 us
    pallas_call x1, Pallas kernels, device_step(): pl.pallas_call(copy_kernel, name='emit', in_specs=[ANY] * 5, out_specs=[A...  9.61 us

profile of v4, /device:TPU:0, one launch (start us, length us, event | category | flops | bytes accessed | tf_op | source)
XLA Modules:
  0.0 181.8 jit_solution(16495814018292610561)
XLA Ops:
  0.6 171.3 %layer.1 = (bf16[1536,2048]{1,0:T(8,128)(2,1)}, bf16[1536,2048]{1,0:T(8,128)(2,1)}, bf16[256,512]{1,0:T(8,128)(2,1)}, bf16[256,512]{1,0:T(8,128)(2,1)}, bf16[512...) custom-call(bf16[1536,2048]{1,0:T(8,128)(2,1)} %x_hbm.1, ...), custom_call_target="tpu_custom_call" | custom-call | flops 80000000000 | bytes 100000000 | tf_op jit(solution)/shard_map/layer/pallas_call | solution.py:628
  172.0 9.6 %emit.1 = (bf16[1536,2048]{1,0:T(8,128)(2,1)}, bf16[1536,2048]{1,0:T(8,128)(2,1)}, bf16[256,512]{1,0:T(8,128)(2,1)}, bf16[256,512]{1,0:T(8,128)(2,1)}, bf16[512,256]{1,0:T(8,128)(2,1)}) custom-call(bf16[1536,2048]{1,0:T(8,128)(2,1)} %get-tuple-element.10.refs_0_, bf16[1536,2048]{1,0:T(8,128)(2,1)} %get-tuple-element.11.refs_1_, ...), custom_call_target="tpu_custom_call" | custom-call | flops 1000000 | bytes 27000000 | tf_op jit(solution)/shard_map/emit/pallas_call | solution.py:638

commit v5 on v4

--- a/solution.py
+++ b/solution.py
@@ -10,6 +10,7 @@
 NORM_EPS = 1e-6
 ROWS = 512
 TOKS = 1536
+TILES = 3
 SEQ = 128
 D = 2048
 CORE = 768
@@ -275,11 +276,12 @@
 
     wq_sh = share(wq, wq_all, colslot(m))
 
-    @pl.loop(0, 3)
+    @pl.loop(0, TILES)
     def _(t):
         r = cols(t, ROWS)
         q[r, :] = dot(xh[r, :], wq[...]).astype(BF)
 
+    relay((3,), 1)
     keep((1,), 2)
     take_all((1,), 3)
     ys[3, None][0].start()
@@ -288,7 +290,7 @@
     for key in keys:
         on(None if key is None else got(*key), lambda key=key: [cs[a, key][1].wait_recv() for a in (1, 2)] and None)
 
-    @pl.loop(0, 3)
+    @pl.loop(0, TILES)
     def _(t):
         r = cols(t, ROWS)
         k[r, :] = dot(xh[r, :], wkv[0]).astype(BF)
@@ -302,7 +304,7 @@
     mask = (posm <= posm.T).astype(F32)
     mask2 = jnp.concatenate([mask, mask], axis=0)
 
-    @pl.loop(0, 3)
+    @pl.loop(0, TILES)
     def _(t):
         rows = [cols(t * 4 + b, SEQ) for b in range(4)]
         qs = [stack_heads(q[r, :]) for r in rows]
@@ -360,11 +362,11 @@
         def _(i):
             kk = 2 + i + (i // 2) * (1 - 2 * i)
             far[g][kk] = piece(g, ((z + kk) % 4) * 2 + 1 - y)
-            ysend(g, kk).start()
-
-    def near(g, kk):
+            pl.when(jnp.logical_or(kk > 0, g == 1))(lambda: ysend(g, kk).start())
+
+    def near(g, kk, part=None):
         ysend(g, kk).wait_recv()
-        ry[g][kk] = ry[g][kk] + piece(g, zpeer[kk])
+        ry[g][kk] = ry[g][kk] + (piece(g, zpeer[kk]) if part is None else part[...])
         if kk == 2 or kk and g == 1:
             zsend(g, kk).start()
         elif kk:
@@ -379,9 +381,10 @@
             total = total + rz[g][2]
         st[...] = total.astype(BF)
 
+    relay((3,), 2)
     send_far(2, 0, 4)
-    relay((3, 4), 1)
-    relay((3, 4), 2)
+    relay((4,), 1)
+    relay((4,), 2)
     near(2, 2)
     keep((3, 4), 1)
     keep((3, 4), 2)
@@ -398,14 +401,14 @@
             dkv[r, :H] = dkv[r, :H] + dks[b] if add else dks[b]
             dkv[r, H:] = dkv[r, H:] + dvs[b] if add else dvs[b]
 
-    @pl.loop(0, 3)
+    @pl.loop(0, TILES)
     def _(t):
         do = dot_t(big[cols(t, ROWS), :], wo[...]).astype(BF)
         qs = [stack_heads(q[cols(t * 4 + b, SEQ), :]) for b in range(4)]
         back_tile(t, qs, [probs[t * 4 + b] for b in range(4)], do, False)
 
     dq_sh = share_rows(dq, dq_all, m)
-    send_far(0, 0, 3)
+    send_far(0, 0, 4)
     near(2, 3)
     near(2, 1)
     merge(2)
@@ -414,7 +417,7 @@
         on(None if key is None else got(*key), lambda key=key: [xs[a, key][1].wait_recv() for a in (0, 5)] and None)
     wqx_sh = share(wqx, wq_all, colslot(across))
 
-    @pl.loop(0, 3)
+    @pl.loop(0, TILES)
     def _(t):
         rows = [cols(t * 4 + b, SEQ) for b in range(4)]
         qm = dot(xh[cols(t, ROWS), :], wqx[...]).astype(BF)
@@ -437,7 +440,7 @@
             device_id={"model": mate}, device_id_type=MESH,
         )
 
-    @pl.loop(0, 3)
+    @pl.loop(0, TILES)
     def _(t):
         do = dot_t(big[cols(t, ROWS), :], wox[...]).astype(BF)
         qs = [stack_heads(dqx[cols(t * 4 + b, SEQ), :]) for b in range(4)]
@@ -458,8 +461,10 @@
         if t == 0:
             tiles[2].start()
     send_far(1, 0, 4)
-    send_far(0, 3, 4)
-    near(2, 0)
+    ysend(2, 0).start()
+    ysend(0, 0).start()
+    last = dkvt.at[0, :, pl.ds(0, H)]
+    last[...] = piece(2, zpeer[0])
     near(0, 2)
 
     for sh in (wo_sh, wox_sh, o_sh, ox_sh):
@@ -534,7 +539,7 @@
             done[0][1].wait_send()
             sends[:] = [s for s in sends if s[1] is not done[0][1]]
 
-        @pl.loop(0, 3)
+        @pl.loop(0, TILES)
         def _(i):
             n, inv = norm(wox[cols(i, SEQ), :].astype(F32))
             gn = jnp.concatenate([dkv[pl.ds(pl.multiple_of(c * PASS + i * SEQ, SEQ), SEQ), :] for c in range(4)], axis=1) * gain[...]
@@ -547,18 +552,19 @@
                 near(1, kk)
     emit(dx_out)
 
-    finish(2, go_st)
-    fin = [local(go_st, go_out)]
+    finish(1, gk_st)
+    fin = [local(gk_st, gkv_out.at[:, cols(m, SEQ)])]
     fin[0].start()
-    finish(1, gk_st)
-    fin.append(local(gk_st, gkv_out.at[:, cols(m, SEQ)]))
-    fin[1].start()
     backs = []
     for peer in (mate, across, diag):
         out, back = remote(gk_st, gkv_out.at[:, cols(m, SEQ)], gkv_out.at[:, cols(peer, SEQ)], "model", peer)
         out.start()
         backs.append(back)
 
+    near(2, 0, last)
+    finish(2, go_st)
+    fin.append(local(go_st, go_out))
+    fin[1].start()
     near(0, 0)
     finish(0, gq_st)
     fin.append(local(gq_st, gq_out))

time: 182 us -> 178 us (0.978)
  Pallas kernels: 181 us -> 177 us
    pallas_call x1, Pallas kernels: 171 us -> 168 us  [device_step(): pl.pallas_call(layer_kernel, name='layer', in_specs=[ANY, IN_VM, ANY, ANY...]
where the time goes in v5:
time: 178 us
  Pallas kernels  177 us (99%)
    pallas_call x1, Pallas kernels, device_step(): pl.pallas_call(layer_kernel, name='layer', in_specs=[ANY, IN_VM, ANY, ANY...  168 us
    pallas_call x1, Pallas kernels, device_step(): pl.pallas_call(copy_kernel, name='emit', in_specs=[ANY] * 5, out_specs=[A...  9.61 us

profile of v5, /device:TPU:0, one launch (start us, length us, event | category | flops | bytes accessed | tf_op | source)
XLA Modules:
  0.0 178.0 jit_solution(8485448404426429545)
XLA Ops:
  0.6 167.6 %layer.1 = (bf16[1536,2048]{1,0:T(8,128)(2,1)}, bf16[1536,2048]{1,0:T(8,128)(2,1)}, bf16[256,512]{1,0:T(8,128)(2,1)}, bf16[256,512]{1,0:T(8,128)(2,1)}, bf16[512...) custom-call(bf16[1536,2048]{1,0:T(8,128)(2,1)} %x_hbm.1, ...), custom_call_target="tpu_custom_call" | custom-call | flops 80000000000 | bytes 100000000 | tf_op jit(solution)/shard_map/layer/pallas_call | solution.py:634
  168.2 9.6 %emit.1 = (bf16[1536,2048]{1,0:T(8,128)(2,1)}, bf16[1536,2048]{1,0:T(8,128)(2,1)}, bf16[256,512]{1,0:T(8,128)(2,1)}, bf16[256,512]{1,0:T(8,128)(2,1)}, bf16[512,256]{1,0:T(8,128)(2,1)}) custom-call(bf16[1536,2048]{1,0:T(8,128)(2,1)} %get-tuple-element.10.refs_0_, bf16[1536,2048]{1,0:T(8,128)(2,1)} %get-tuple-element.11.refs_1_, ...), custom_call_target="tpu_custom_call" | custom-call | flops 1000000 | bytes 27000000 | tf_op jit(solution)/shard_map/emit/pallas_call | solution.py:644

commit v6 on v5

--- a/solution.py
+++ b/solution.py
@@ -429,6 +429,7 @@
             ox[rows[b], :] = spread_heads(os[b])
 
     ox_sh = share_rows(ox, o_all, across)
+    near(0, 2)
     for key in keys:
         on(None if key is None else got(*key), lambda key=key: [xs[a, key][1].wait_recv() for a in (3, 4)] and None)
     wox_sh = share(wox, wo_all, rowslot(across))
@@ -465,7 +466,7 @@
     ysend(0, 0).start()
     last = dkvt.at[0, :, pl.ds(0, H)]
     last[...] = piece(2, zpeer[0])
-    near(0, 2)
+    near(0, 3)
 
     for sh in (wo_sh, wox_sh, o_sh, ox_sh):
         sh[0].wait()
@@ -496,7 +497,8 @@
         fill[i].wait()
         y_cols(2 * i, 2 * i + 2)
         if i == 1:
-            near(0, 3)
+            near(0, 1)
+            merge(0)
     emit(y_out)
 
     for sh in (wq_sh, wqx_sh, dq_sh, dqx_sh):
@@ -514,8 +516,6 @@
     xin[0].start()
     for t in range(3):
         dkv_send(t).wait_send()
-    near(0, 1)
-    merge(0)
     fetch.wait()
     for p in range(2):
         rows = pl.ds(pl.multiple_of(core * CORE + p * PASS, PASS), PASS)

time: 178 us -> 172 us (0.966)
  Pallas kernels: 177 us -> 170 us
    pallas_call x1, Pallas kernels: 168 us -> 160 us  [device_step(): pl.pallas_call(layer_kernel, name='layer', in_specs=[ANY, IN_VM, ANY, ANY...]
where the time goes in v6:
time: 172 us; the launch traced here: 171 us
  Pallas kernels  170 us (99%)
    pallas_call x1, Pallas kernels, device_step(): pl.pallas_call(layer_kernel, name='layer', in_specs=[ANY, IN_VM, ANY, ANY...  160 us
    pallas_call x1, Pallas kernels, device_step(): pl.pallas_call(copy_kernel, name='emit', in_specs=[ANY] * 5, out_specs=[A...  9.61 us

profile of v6, /device:TPU:0, one launch (start us, length us, event | category | flops | bytes accessed | tf_op | source)
XLA Modules:
  0.0 170.7 jit_solution(2765079339265987384)
XLA Ops:
  0.6 160.3 %layer.1 = (bf16[1536,2048]{1,0:T(8,128)(2,1)}, bf16[1536,2048]{1,0:T(8,128)(2,1)}, bf16[256,512]{1,0:T(8,128)(2,1)}, bf16[256,512]{1,0:T(8,128)(2,1)}, bf16[512...) custom-call(bf16[1536,2048]{1,0:T(8,128)(2,1)} %x_hbm.1, ...), custom_call_target="tpu_custom_call" | custom-call | flops 80000000000 | bytes 100000000 | tf_op jit(solution)/shard_map/layer/pallas_call | solution.py:634
  160.9 9.6 %emit.1 = (bf16[1536,2048]{1,0:T(8,128)(2,1)}, bf16[1536,2048]{1,0:T(8,128)(2,1)}, bf16[256,512]{1,0:T(8,128)(2,1)}, bf16[256,512]{1,0:T(8,128)(2,1)}, bf16[512,256]{1,0:T(8,128)(2,1)}) custom-call(bf16[1536,2048]{1,0:T(8,128)(2,1)} %get-tuple-element.10.refs_0_, bf16[1536,2048]{1,0:T(8,128)(2,1)} %get-tuple-element.11.refs_1_, ...), custom_call_target="tpu_custom_call" | custom-call | flops 1000000 | bytes 27000000 | tf_op jit(solution)/shard_map/emit/pallas_call | solution.py:644

commit v7 on v6

--- a/solution.py
+++ b/solution.py
@@ -11,6 +11,7 @@
 ROWS = 512
 TOKS = 1536
 TILES = 3
+SEQS = 4
 SEQ = 128
 D = 2048
 CORE = 768
@@ -92,7 +93,7 @@
     d, m = lax.axis_index("data"), lax.axis_index("model")
     z, y = d // 2, d % 2
     core = m % 2
-    zpeer = [((z + s) % 4) * 2 + y for s in range(4)]
+    zpeer = [((z + s) % 4) * 2 + y for s in range(SEQS)]
     ypeer = z * 2 + 1 - y
     mate = m + 1 - 2 * core
     across = (m + 2) % 4
@@ -234,11 +235,11 @@
         on(None if key is None else got(*key), go)
 
     take_all((0,), 1)
-    take_all((0,), 2)
     for way in WAYS:
         start_hop(1, way, 1)
+    take_all((0,), 2)
+    take_all((1,), 1)
     take_all((0,), 3)
-    take_all((1,), 1)
     for key in keys[:5]:
         arrive(0, key)
     relay((1,), 2)
@@ -306,10 +307,10 @@
 
     @pl.loop(0, TILES)
     def _(t):
-        rows = [cols(t * 4 + b, SEQ) for b in range(4)]
+        rows = [cols(t * 4 + b, SEQ) for b in range(SEQS)]
         qs = [stack_heads(q[r, :]) for r in rows]
         ps, os = attend(qs, [k[r, :] for r in rows], [v[r, :] for r in rows], mask2)
-        for b in range(4):
+        for b in range(SEQS):
             probs[t * 4 + b] = ps[b]
             wide = spread_heads(os[b])
             o[rows[b], :] = wide
@@ -392,9 +393,9 @@
     wo_sh = share(wo, wo_all, rowslot(m))
 
     def back_tile(t, q_of, ps, do, add):
-        rows = [cols(t * 4 + b, SEQ) for b in range(4)]
+        rows = [cols(t * 4 + b, SEQ) for b in range(SEQS)]
         qs, ks, vs = q_of, [k[r, :] for r in rows], [v[r, :] for r in rows]
-        dqs, dks, dvs = attend_back(qs, ks, vs, ps, [stack_heads(do[b * SEQ : (b + 1) * SEQ]) for b in range(4)])
+        dqs, dks, dvs = attend_back(qs, ks, vs, ps, [stack_heads(do[b * SEQ : (b + 1) * SEQ]) for b in range(SEQS)])
         to = dqx if add else dq
         for b, r in enumerate(rows):
             to[r, :] = spread_heads(dqs[b])
@@ -404,8 +405,8 @@
     @pl.loop(0, TILES)
     def _(t):
         do = dot_t(big[cols(t, ROWS), :], wo[...]).astype(BF)
-        qs = [stack_heads(q[cols(t * 4 + b, SEQ), :]) for b in range(4)]
-        back_tile(t, qs, [probs[t * 4 + b] for b in range(4)], do, False)
+        qs = [stack_heads(q[cols(t * 4 + b, SEQ), :]) for b in range(SEQS)]
+        back_tile(t, qs, [probs[t * 4 + b] for b in range(SEQS)], do, False)
 
     dq_sh = share_rows(dq, dq_all, m)
     send_far(0, 0, 4)
@@ -419,12 +420,12 @@
 
     @pl.loop(0, TILES)
     def _(t):
-        rows = [cols(t * 4 + b, SEQ) for b in range(4)]
+        rows = [cols(t * 4 + b, SEQ) for b in range(SEQS)]
         qm = dot(xh[cols(t, ROWS), :], wqx[...]).astype(BF)
-        qs = [stack_heads(qm[b * SEQ : (b + 1) * SEQ]) for b in range(4)]
+        qs = [stack_heads(qm[b * SEQ : (b + 1) * SEQ]) for b in range(SEQS)]
         ps, os = attend(qs, [k[r, :] for r in rows], [v[r, :] for r in rows], mask2)
         dqx[cols(t, ROWS), :] = qm
-        for b in range(4):
+        for b in range(SEQS):
             probs[t * 4 + b] = ps[b]
             ox[rows[b], :] = spread_heads(os[b])
 
@@ -444,8 +445,8 @@
     @pl.loop(0, TILES)
     def _(t):
         do = dot_t(big[cols(t, ROWS), :], wox[...]).astype(BF)
-        qs = [stack_heads(dqx[cols(t * 4 + b, SEQ), :]) for b in range(4)]
-        back_tile(t, qs, [probs[t * 4 + b] for b in range(4)], do, True)
+        qs = [stack_heads(dqx[cols(t * 4 + b, SEQ), :]) for b in range(SEQS)]
+        back_tile(t, qs, [probs[t * 4 + b] for b in range(SEQS)], do, True)
         dkv_send(t).start()
 
     dqx_sh = share_rows(dqx, dq_all, across)
@@ -474,7 +475,7 @@
         drop(locals_, sh[0])
     fetch = local(o_all, tin)
     fetch.start()
-    fill = [local(wo_all.at[:, cols(i, W)], big.at[:, cols(i, W)]) for i in range(4)]
+    fill = [local(wo_all.at[:, cols(i, W)], big.at[:, cols(i, W)]) for i in range(SEQS)]
     for c in fill:
         c.start()
     fetch.wait()
@@ -493,7 +494,7 @@
         out.start()
         done.append((c, out, back))
 
-    for i in range(4):
+    for i in range(SEQS):
         fill[i].wait()
         y_cols(2 * i, 2 * i + 2)
         if i == 1:
@@ -507,7 +508,7 @@
         drop(locals_, sh[0])
     fetch = local(dq_all, tin)
     fetch.start()
-    fill = [local(wq_all.at[cols(i, W)], big.at[cols(i, W)]) for i in range(4)]
+    fill = [local(wq_all.at[cols(i, W)], big.at[cols(i, W)]) for i in range(SEQS)]
     for c in fill:
         c.start()
     wox_sh[1].wait_send()
@@ -527,7 +528,7 @@
             dkv[cols(i, PASS), :] = g + dot_t(q[rows, H:], wkv[1, c, :])
 
         if p == 0:
-            for n in range(4):
+            for n in range(SEQS):
                 fill[n].wait()
                 pl.loop(n, n + 1)(dh_cols)
         else:
@@ -542,7 +543,7 @@
         @pl.loop(0, TILES)
         def _(i):
             n, inv = norm(wox[cols(i, SEQ), :].astype(F32))
-            gn = jnp.concatenate([dkv[pl.ds(pl.multiple_of(c * PASS + i * SEQ, SEQ), SEQ), :] for c in range(4)], axis=1) * gain[...]
+            gn = jnp.concatenate([dkv[pl.ds(pl.multiple_of(c * PASS + i * SEQ, SEQ), SEQ), :] for c in range(SEQS)], axis=1) * gain[...]
             g = inv * (gn - jnp.mean(gn, axis=-1, keepdims=True) - n * jnp.mean(gn * n, axis=-1, keepdims=True))
             stage[pl.ds(pl.multiple_of(p * PASS + i * SEQ, SEQ), SEQ), :] = g.astype(BF)
 
@@ -551,6 +552,8 @@
             for kk in (2, 3, 1, 0):
                 near(1, kk)
     emit(dx_out)
+    lastq = dkvt.at[1, pl.ds(0, H)]
+    lastq[...] = piece(0, zpeer[0])
 
     finish(1, gk_st)
     fin = [local(gk_st, gkv_out.at[:, cols(m, SEQ)])]
@@ -565,7 +568,7 @@
     finish(2, go_st)
     fin.append(local(go_st, go_out))
     fin[1].start()
-    near(0, 0)
+    near(0, 0, lastq)
     finish(0, gq_st)
     fin.append(local(gq_st, gq_out))
     fin[2].start()
@@ -579,7 +582,7 @@
     for c in locals_ + fin:
         c.wait()
     for g in range(3):
-        for kk in range(4):
+        for kk in range(SEQS):
             ysend(g, kk).wait_send()
             if kk:
                 zsend(g, kk).wait_send()

time: 172 us -> 172 us (level)
  no operation moved by 1% of the time
where the time goes in v7:
time: 172 us
  Pallas kernels  171 us (99%)
    pallas_call x1, Pallas kernels, device_step(): pl.pallas_call(layer_kernel, name='layer', in_specs=[ANY, IN_VM, ANY, ANY...  161 us
    pallas_call x1, Pallas kernels, device_step(): pl.pallas_call(copy_kernel, name='emit', in_specs=[ANY] * 5, out_specs=[A...  9.61 us

profile of v7, /device:TPU:0, one launch (start us, length us, event | category | flops | bytes accessed | tf_op | source)
XLA Modules:
  0.0 171.8 jit_solution(17103042384502991715)
XLA Ops:
  0.6 161.4 %layer.1 = (bf16[1536,2048]{1,0:T(8,128)(2,1)}, bf16[1536,2048]{1,0:T(8,128)(2,1)}, bf16[256,512]{1,0:T(8,128)(2,1)}, bf16[256,512]{1,0:T(8,128)(2,1)}, bf16[512...) custom-call(bf16[1536,2048]{1,0:T(8,128)(2,1)} %x_hbm.1, ...), custom_call_target="tpu_custom_call" | custom-call | flops 80000000000 | bytes 100000000 | tf_op jit(solution)/shard_map/layer/pallas_call | solution.py:637
  162.0 9.6 %emit.1 = (bf16[1536,2048]{1,0:T(8,128)(2,1)}, bf16[1536,2048]{1,0:T(8,128)(2,1)}, bf16[256,512]{1,0:T(8,128)(2,1)}, bf16[256,512]{1,0:T(8,128)(2,1)}, bf16[512,256]{1,0:T(8,128)(2,1)}) custom-call(bf16[1536,2048]{1,0:T(8,128)(2,1)} %get-tuple-element.10.refs_0_, bf16[1536,2048]{1,0:T(8,128)(2,1)} %get-tuple-element.11.refs_1_, ...), custom_call_target="tpu_custom_call" | custom-call | flops 1000000 | bytes 27000000 | tf_op jit(solution)/shard_map/emit/pallas_call | solution.py:647

commit v8 on v7

--- a/solution.py
+++ b/solution.py
@@ -350,13 +350,12 @@
             return zcopy(g, kk, 2, zpeer[2])
         return zcopy(g, kk, kk // 2, zpeer[kk])
 
-    def merge(g):
+    def merge(g, kk):
         @pl.when(inner)
         def _():
-            for kk in (3, 1):
-                zcopy(g, 2, 2 + kk // 2, ypeer).wait_recv()
-                ry[g][kk] = ry[g][kk] + rz[g][2 + kk // 2]
-                zsend(g, kk).start()
+            zcopy(g, 2, 2 + kk // 2, ypeer).wait_recv()
+            ry[g][kk] = ry[g][kk] + rz[g][2 + kk // 2]
+            zsend(g, kk).start()
 
     def send_far(g, lo, hi):
         @pl.loop(lo, hi)
@@ -411,8 +410,9 @@
     dq_sh = share_rows(dq, dq_all, m)
     send_far(0, 0, 4)
     near(2, 3)
+    merge(2, 3)
     near(2, 1)
-    merge(2)
+    merge(2, 1)
 
     for key in keys:
         on(None if key is None else got(*key), lambda key=key: [xs[a, key][1].wait_recv() for a in (0, 5)] and None)
@@ -468,6 +468,7 @@
     last = dkvt.at[0, :, pl.ds(0, H)]
     last[...] = piece(2, zpeer[0])
     near(0, 3)
+    merge(0, 3)
 
     for sh in (wo_sh, wox_sh, o_sh, ox_sh):
         sh[0].wait()
@@ -499,7 +500,7 @@
         y_cols(2 * i, 2 * i + 2)
         if i == 1:
             near(0, 1)
-            merge(0)
+            merge(0, 1)
     emit(y_out)
 
     for sh in (wq_sh, wqx_sh, dq_sh, dqx_sh):

time: 172 us -> 172 us (level)
  no operation moved by 1% of the time
where the time goes in v8:
time: 172 us
  Pallas kernels  171 us (99%)
    pallas_call x1, Pallas kernels, device_step(): pl.pallas_call(layer_kernel, name='layer', in_specs=[ANY, IN_VM, ANY, ANY...  161 us
    pallas_call x1, Pallas kernels, device_step(): pl.pallas_call(copy_kernel, name='emit', in_specs=[ANY] * 5, out_specs=[A...  9.61 us

profile of v8, /device:TPU:0, one launch (start us, length us, event | category | flops | bytes accessed | tf_op | source)
XLA Modules:
  0.0 171.8 jit_solution(14652104687025281786)
XLA Ops:
  0.6 161.4 %layer.1 = (bf16[1536,2048]{1,0:T(8,128)(2,1)}, bf16[1536,2048]{1,0:T(8,128)(2,1)}, bf16[256,512]{1,0:T(8,128)(2,1)}, bf16[256,512]{1,0:T(8,128)(2,1)}, bf16[512...) custom-call(bf16[1536,2048]{1,0:T(8,128)(2,1)} %x_hbm.1, ...), custom_call_target="tpu_custom_call" | custom-call | flops 80000000000 | bytes 100000000 | tf_op jit(solution)/shard_map/layer/pallas_call | solution.py:638
  162.0 9.6 %emit.1 = (bf16[1536,2048]{1,0:T(8,128)(2,1)}, bf16[1536,2048]{1,0:T(8,128)(2,1)}, bf16[256,512]{1,0:T(8,128)(2,1)}, bf16[256,512]{1,0:T(8,128)(2,1)}, bf16[512,256]{1,0:T(8,128)(2,1)}) custom-call(bf16[1536,2048]{1,0:T(8,128)(2,1)} %get-tuple-element.10.refs_0_, bf16[1536,2048]{1,0:T(8,128)(2,1)} %get-tuple-element.11.refs_1_, ...), custom_call_target="tpu_custom_call" | custom-call | flops 1000000 | bytes 27000000 | tf_op jit(solution)/shard_map/emit/pallas_call | solution.py:648
